TPU v7x, 8 devices: a whole 2x2x1 slice. The times are simulated.
8 devices in a mesh: dp: 1 (over z), cp: 8 (over y, x, core).
Axes of the slice: x: 2, y: 2, z: 1, core: 2. Of those that a mesh axis runs over, the one named last changes fastest.
Arguments:
- x_in: bfloat16 [1536, 3584], P(('dp', 'cp'))
- dy_in: bfloat16 [1536, 3584], P(('dp', 'cp'))
- doc_id: int32 [1536], P(('dp', 'cp'))
- w_q: bfloat16 [3584, 7, 128], replicated
- w_k: bfloat16 [3584, 1, 128], replicated
- w_v: bfloat16 [3584, 1, 128], replicated
- w_o: bfloat16 [7, 128, 3584], replicated
Outputs:
- output 1: bfloat16 [1536, 3584], P(('dp', 'cp'))
- output 2: bfloat16 [1536, 3584], P(('dp', 'cp'))
All inputs are finite; a program needn't handle non-finite values.
Results may differ from a plain program's by a relative error of at most 0.00949353.
Values are sent between devices in bfloat16 or wider.
A program may use at most 1 GiB of HBM per device.

v0:
```python
import jax
import jax.numpy as jnp
from jax import lax
from jax.sharding import PartitionSpec as P

NEG_BIG = -1.0e30


def stored_positions(seq_len, group_devs):
    tok_dev = seq_len // group_devs
    piece_len = tok_dev // 2
    row_idx = jnp.arange(seq_len, dtype=jnp.int32)
    owner_dev = row_idx // tok_dev
    offset = row_idx % tok_dev
    piece_idx = jnp.where(offset < piece_len, owner_dev, 2 * group_devs - 1 - owner_dev)
    return piece_idx * piece_len + offset % piece_len


def solution(mesh):
    group_devs = mesh.shape['cp']
    row_spec = P(('dp', 'cp'))
    full_spec = P()

    def local_layer(x_in, dy_in, doc_id, w_q, w_k, w_v, w_o):
        tok_dev, d_model = x_in.shape
        q_heads, head_dim = w_q.shape[1], w_q.shape[2]
        kv_heads = w_k.shape[1]
        q_group = q_heads // kv_heads
        seq_len = tok_dev * group_devs
        score_scale = head_dim ** -0.5
        wq_grp = w_q.reshape(d_model, kv_heads, q_group, head_dim)
        wo_grp = w_o.reshape(kv_heads, q_group, head_dim, d_model)
        all_pos = stored_positions(seq_len, group_devs)
        my_pos = lax.dynamic_slice_in_dim(all_pos, lax.axis_index('cp') * tok_dev, tok_dev)
        q_loc = jnp.einsum('td,dkge->tkge', x_in, wq_grp, preferred_element_type=jnp.float32).astype(jnp.bfloat16)
        k_loc = jnp.einsum('td,dke->tke', x_in, w_k, preferred_element_type=jnp.float32).astype(jnp.bfloat16)
        v_loc = jnp.einsum('td,dke->tke', x_in, w_v, preferred_element_type=jnp.float32).astype(jnp.bfloat16)
        k_all = lax.all_gather(k_loc, 'cp', axis=0, tiled=True)
        v_all = lax.all_gather(v_loc, 'cp', axis=0, tiled=True)
        doc_all = lax.all_gather(doc_id, 'cp', axis=0, tiled=True)
        visible = (all_pos[None, :] <= my_pos[:, None]) & (doc_all[None, :] == doc_id[:, None])
        scores = jnp.einsum('tkge,ske->tkgs', q_loc, k_all, preferred_element_type=jnp.float32) * score_scale
        scores = jnp.where(visible[:, None, None, :], scores, NEG_BIG)
        log_norm = jax.nn.logsumexp(scores, axis=-1, keepdims=True)
        prob_bf = jnp.exp(scores - log_norm).astype(jnp.bfloat16)
        out_loc = jnp.einsum('tkgs,ske->tkge', prob_bf, v_all, preferred_element_type=jnp.float32).astype(jnp.bfloat16)
        y_out = jnp.einsum('tkge,kged->td', out_loc, wo_grp, preferred_element_type=jnp.float32).astype(jnp.bfloat16)
        do_loc = jnp.einsum('td,kged->tkge', dy_in, wo_grp, preferred_element_type=jnp.float32).astype(jnp.bfloat16)
        delta_row = jnp.einsum('tkge,tkge->tkg', do_loc, out_loc, preferred_element_type=jnp.float32)
        d_prob = jnp.einsum('tkge,ske->tkgs', do_loc, v_all, preferred_element_type=jnp.float32)
        d_score = (prob_bf.astype(jnp.float32) * (d_prob - delta_row[:, :, :, None])).astype(jnp.bfloat16)
        dq_loc = (jnp.einsum('tkgs,ske->tkge', d_score, k_all, preferred_element_type=jnp.float32) * score_scale).astype(jnp.bfloat16)
        dk_part = jnp.einsum('tkgs,tkge->ske', d_score, q_loc, preferred_element_type=jnp.float32) * score_scale
        dv_part = jnp.einsum('tkgs,tkge->ske', prob_bf, do_loc, preferred_element_type=jnp.float32)
        dk_loc = lax.psum_scatter(dk_part, 'cp', scatter_dimension=0, tiled=True)
        dv_loc = lax.psum_scatter(dv_part, 'cp', scatter_dimension=0, tiled=True)
        dx_wide = (jnp.einsum('tkge,dkge->td', dq_loc, wq_grp, preferred_element_type=jnp.float32)
                   + jnp.einsum('tke,dke->td', dk_loc.astype(jnp.bfloat16), w_k, preferred_element_type=jnp.float32)
                   + jnp.einsum('tke,dke->td', dv_loc.astype(jnp.bfloat16), w_v, preferred_element_type=jnp.float32))
        return y_out, dx_wide.astype(jnp.bfloat16)

    return jax.shard_map(local_layer, mesh=mesh,
                         in_specs=(row_spec, row_spec, row_spec, full_spec, full_spec, full_spec, full_spec),
                         out_specs=(row_spec, row_spec), check_vma=False)
```

profile of v0, /device:TPU:0, one launch (start us, length us, event | category | flops | bytes accessed | tf_op | source)
XLA Modules:
  0.0 147.6 jit_solution(258905618632475438)
XLA Ops:
  7.2 0.0 copy-start
  7.2 0.0 reduce-scatter.3.cloned.1.call-start
  7.3 1.0 dynamic-update-slice
  8.2 25.1 %all-reduce = s32[1536]{0:T(1024)S(1)} all-reduce(s32[1536]{0:T(1024)S(1)} %dynamic-update-slice), channel_id=1, replica_groups=mesh['dp'=1,'cp'=8] {'cp'}, use_global_device_ids=true, to_apply=%add | all-reduce | flops 1536 | bytes 12288
  33.3 1.7 %convolution_convert_fusion = bf16[192,128]{1,0:T(8,128)(2,1)S(1)} fusion(bf16[192,3584]{1,0:T(8,128)(2,1)S(1)} %copy-done, bf16[3584,1,128]{2,0,1:T(8,128)(2,1)} %param.11), kind=kOutput, calls=%fused_computation.37 | convolution fusion | flops 176185344 | bytes 2342912 | tf_op jit(solution)/shard_map/td,dke->tke/dot_general | solution.py:36
  35.0 12.7 %all-gather.1 = bf16[1536,128]{1,0:T(8,128)(2,1)S(1)} all-gather(bf16[192,128]{1,0:T(8,128)(2,1)S(1)} %convolution_convert_fusion), channel_id=3, replica_groups=mesh['dp'=1,'cp'=8] {'cp'}, dimensions={0}, use_global_device_ids=true | all-gather | bytes 442368 | tf_op jit(solution)/shard_map/all_gather | solution.py:38
  47.8 4.6 %fusion.34 = bf16[192,7,128]{2,0,1:T(8,128)(2,1)S(1)} fusion(bf16[3584,7,128]{2,0,1:T(8,128)(2,1)} %param.10, bf16[192,3584]{1,0:T(8,128)(2,1)S(1)} %copy-done), kind=kOutput, calls=%fused_computation.31 | convolution fusion | flops 1233297408 | bytes 8142848 | tf_op jit(solution)/shard_map/td,dkge->tkge/dot_general | solution.py:35
  52.4 0.1 dynamic_slice.3
  52.4 0.3 compare_and_fusion
  52.8 1.7 %fusion.1 = (f32[192,7]{0,1:T(8,128)S(1)}, f32[1536,192,7]{0,1,2:T(8,128)S(1)}) fusion(pred[192,1536]{1,0:T(8,128)(4,1)S(1)} %compare_and_fusion, bf16[192,7,128]{2,0,1:T(8,128)(2,1)S(1)} %fusion.34, bf16[1536,128]{1,0:T(8,128)(2,1)S(1)} %all-gather.1), kind=kOutput, calls=%fused_computation.6 | convolution fusion | flops 534674112 | bytes 9295104 | tf_op jit(solution)/shard_map/tkge,ske->tkgs/dot_general | solution.py:42
  54.5 2.2 %exponential_reduce_fusion = f32[192,7]{0,1:T(8,128)S(1)} fusion(f32[1536,192,7]{0,1,2:T(8,128)S(1)} %get-tuple-element.3, f32[192,7]{0,1:T(8,128)S(1)} %is-finite_select_fusion, pred[192,1536]{1,0:T(8,128)(4,1)S(1)} %compare_and_fusion), kind=kLoop, calls=%fused_computation.5 | loop fusion | flops 8256192 | bytes 8563200 | tf_op jit(solution)/shard_map/reduce_sum | solution.py:44
  56.7 0.0 slice-start.1
  56.7 1.8 %exponential_convert_fusion = bf16[192,1,7,1536]{3,0,2,1:T(8,128)(2,1)S(1)} fusion(f32[1536,192,7]{0,1,2:T(8,128)S(1)} %get-tuple-element.3, f32[192,7]{0,1:T(8,128)S(1)} %log_add_fusion, pred[192,1536]{1,0:T(8,128)(4,1)S(1)} %compare_and_fusion), kind=kLoop, calls=%fused_computation.4 | loop fusion | flops 8257536 | bytes 12686592 | tf_op jit(solution)/shard_map/convert_element_type | solution.py:45
  58.5 0.5 convolution_convert_fusion.1
  59.0 12.4 %all-gather = bf16[1536,128]{1,0:T(8,128)(2,1)S(1)} all-gather(bf16[192,128]{1,0:T(8,128)(2,1)S(1)} %convolution_convert_fusion.1), channel_id=2, replica_groups=mesh['dp'=1,'cp'=8] {'cp'}, dimensions={0}, use_global_device_ids=true | all-gather | bytes 442368 | tf_op jit(solution)/shard_map/all_gather | solution.py:39
  71.5 1.3 fusion.43
  72.8 2.4 %fusion.55 = (f32[192,7]{0,1:T(8,128)S(1)}, bf16[192,7,128]{2,0,1:T(8,128)(2,1)S(1)}) fusion(bf16[192,7,128]{2,0,1:T(8,128)(2,1)S(1)} %fusion.43, bf16[7,128,3584]{2,1,0:T(8,128)(2,1)S(1)} %bitcast.140, bf16[192,3584]{1,0:T(8,128)(2,1)S(1)} %copy-done.10), kind=kOutput, calls=%fused_computation.44 | convolution fusion | flops 1233984256 | bytes 8492288 | tf_op jit(solution)/shard_map/td,kged->tkge/dot_general | solution.py:48
  75.2 1.3 fusion
  76.5 1.9 %copy-done.2 = bf16[192,1,7,1536]{3,0,2,1:T(8,128)(2,1)} copy-done((bf16[192,1,7,1536]{3,0,2,1:T(8,128)(2,1)}, bf16[192,1,7,1536]{3,0,2,1:T(8,128)(2,1)S(1)}, u32[]{:S(2)}) %copy-start.2) | copy-done | bytes 4128792
  78.4 0.8 fusion.21
  79.2 1.7 %copy.11 = f32[1536,1,128]{2,1,0:T(1,128)} copy(f32[1536,1,128]{0,2,1:T(8,128)S(1)} %fusion.21) | data formatting | bytes 1572864 | tf_op jit(solution)/shard_map/mul | solution.py:53
  81.0 0.0 reduce-scatter.3.cloned.1.call-update
  81.0 0.0 reduce-scatter.5.cloned.1.call-start
  81.0 3.0 %fusion.12 = f32[1536,1,128]{0,2,1:T(8,128)S(1)} fusion(bf16[192,7,128]{2,0,1:T(8,128)(2,1)S(1)} %get-tuple-element.5, bf16[192,1,7,1536]{3,0,2,1:T(8,128)(2,1)} %copy-done.1), kind=kOutput, calls=%fused_computation.21 | convolution fusion | flops 528482304 | bytes 5259264 | tf_op jit(solution)/shard_map/tkgs,tkge->ske/dot_general | solution.py:54
  84.0 1.7 %copy.13 = f32[1536,1,128]{2,1,0:T(1,128)} copy(f32[1536,1,128]{0,2,1:T(8,128)S(1)} %fusion.12) | data formatting | bytes 1572864 | tf_op jit(solution)/shard_map/tkgs,tkge->ske/transpose | solution.py:54
  85.7 0.0 reduce-scatter.5.cloned.1.call-update
  85.8 5.6 %fusion.2 = bf16[192,3584]{1,0:T(8,128)(2,1)} fusion(bf16[192,7,128]{2,0,1:T(8,128)(2,1)} %copy-done.8, bf16[7,128,3584]{2,1,0:T(8,128)(2,1)} %param.13), kind=kOutput, calls=%fused_computation.11 | convolution fusion | flops 1233813504 | bytes 8142848 | tf_op jit(solution)/shard_map/tkge,kged->td/dot_general | solution.py:47
  91.4 11.0 %convolution_bitcast_fusion = f32[192,3584]{1,0:T(8,128)} fusion(bf16[3584,7,128]{2,0,1:T(8,128)(2,1)} %param.10, bf16[192,1,7,1536]{3,0,2,1:T(8,128)(2,1)} %copy-done.2, bf16[1536,128]{1,0:T(8,128)(2,1)} %copy-done.5), kind=kOutput, calls=%fused_computation.9 | convolution fusion | flops 1761951744 | bytes 13697024 | tf_op jit(solution)/shard_map/tkge,dkge->td/dot_general | solution.py:57
  102.4 5.3 %reduce-scatter.3.cloned.1.call-done = f32[192,1,128]{2,1,0:T(1,128)} async-done(((f32[1536,1,128]{2,1,0:T(1,128)}), f32[192,1,128]{2,1,0:T(1,128)}) %reduce-scatter.3.cloned.1.call-update) | async-done | bytes 98320 | tf_op jit(solution)/shard_map/reduce_scatter | solution.py:55
  107.7 3.9 %convolution_add_fusion.1 = f32[192,3584]{1,0:T(8,128)} fusion(f32[192,3584]{1,0:T(8,128)} %convolution_bitcast_fusion, bf16[3584,1,128]{2,0,1:T(8,128)(2,1)S(1)} %copy-done.3, f32[192,1,128]{2,0,1:T(8,128)} %bitcast.137), kind=kOutput, calls=%fused_computation.8 | convolution fusion | flops 176873472 | bytes 6520832 | tf_op jit(solution)/shard_map/tke,dke->td/dot_general | solution.py:58
  111.6 25.7 %reduce-scatter.5.cloned.1.call-done = f32[192,1,128]{2,1,0:T(1,128)} async-done(((f32[1536,1,128]{2,1,0:T(1,128)}), f32[192,1,128]{2,1,0:T(1,128)}) %reduce-scatter.5.cloned.1.call-update) | async-done | bytes 98320 | tf_op jit(solution)/shard_map/reduce_scatter | solution.py:56
  137.3 3.4 %fusion.3 = bf16[192,3584]{1,0:T(8,128)(2,1)} fusion(f32[192,3584]{1,0:T(8,128)} %convolution_add_fusion.1, bf16[3584,1,128]{2,0,1:T(8,128)(2,1)S(1)} %copy-done.4, f32[192,1,128]{2,0,1:T(8,128)} %bitcast.138), kind=kOutput, calls=%fused_computation.12 | convolution fusion | flops 177561600 | bytes 5144576 | tf_op jit(solution)/shard_map/tke,dke->td/dot_general | solution.py:59
  (28 shorter events, 0.1 us)
Async XLA Ops:
  7.2 26.2 %copy-start = (bf16[192,3584]{1,0:T(8,128)(2,1)S(1)}, bf16[192,3584]{1,0:T(8,128)(2,1)}, u32[]{:S(2)}) copy-start(bf16[192,3584]{1,0:T(8,128)(2,1)} %param.7) | copy-start | bytes 4128772
  7.2 100.5 %reduce-scatter.3.cloned.1.call-start = ((), (), s32[]{:S(2)}) async-start(), calls=%async_computation.2 | async-start | bytes 884736 | tf_op jit(solution)/shard_map/reduce_scatter | solution.py:55
  47.7 5.0 %copy-start.5 = (bf16[1536,128]{1,0:T(8,128)(2,1)}, bf16[1536,128]{1,0:T(8,128)(2,1)S(1)}, u32[]{:S(2)}) copy-start(bf16[1536,128]{1,0:T(8,128)(2,1)S(1)} %all-gather.1) | copy-start | bytes 1179652
  47.8 4.7 %copy-start.9 = (s32[192]{0:T(256)S(1)}, s32[192]{0:T(256)}, u32[]{:S(2)}) copy-start(s32[192]{0:T(256)} %param.9) | copy-start | bytes 2308
  52.3 2.1 %copy-start.6 = (bf16[192,7,128]{2,0,1:T(8,128)(2,1)}, bf16[192,7,128]{2,0,1:T(8,128)(2,1)S(1)}, u32[]{:S(2)}) copy-start(bf16[192,7,128]{2,0,1:T(8,128)(2,1)S(1)} %fusion.34) | copy-start | bytes 1032196
  56.7 16.1 %slice-start = ((s8[6422528]{0:T(1024)(128)(4,1)}), s8[2228224]{0:T(1024)(128)(4,1)S(1)}, s32[]{:S(2)}) async-start(s8[6422528]{0:T(1024)(128)(4,1)} %bitcast.139), calls=%async_computation.4 | async-start | bytes 4456448
  56.7 1.8 %copy-start.4 = (bf16[3584,1,128]{2,0,1:T(8,128)(2,1)S(1)}, bf16[3584,1,128]{2,0,1:T(8,128)(2,1)}, u32[]{:S(2)}) copy-start(bf16[3584,1,128]{2,0,1:T(8,128)(2,1)} %param.12) | copy-start | bytes 2752516
  56.7 16.0 %slice-start.1 = ((s8[6422528]{0:T(1024)(128)(4,1)}), s8[4194304]{0:T(1024)(128)(4,1)S(1)}, s32[]{:S(2)}) async-start(s8[6422528]{0:T(1024)(128)(4,1)} %bitcast.139), calls=%async_computation.5 | async-start | bytes 8388608
  58.5 16.7 %copy-start.1 = (bf16[192,1,7,1536]{3,0,2,1:T(8,128)(2,1)}, bf16[192,1,7,1536]{3,0,2,1:T(8,128)(2,1)S(1)}, u32[]{:S(2)}) copy-start(bf16[192,1,7,1536]{3,0,2,1:T(8,128)(2,1)S(1)} %exponential_convert_fusion) | copy-start | bytes 12386308
  58.5 14.3 %copy-start.10 = (bf16[192,3584]{1,0:T(8,128)(2,1)S(1)}, bf16[192,3584]{1,0:T(8,128)(2,1)}, u32[]{:S(2)}) copy-start(bf16[192,3584]{1,0:T(8,128)(2,1)} %param.8) | copy-start | bytes 4128772
  72.8 2.4 %copy-start.8 = (bf16[192,7,128]{2,0,1:T(8,128)(2,1)}, bf16[192,7,128]{2,0,1:T(8,128)(2,1)S(1)}, u32[]{:S(2)}) copy-start(bf16[192,7,128]{2,0,1:T(8,128)(2,1)S(1)} %fusion.43) | copy-start | bytes 1032196
  75.2 3.2 %copy-start.7 = (bf16[192,7,128]{2,0,1:T(8,128)(2,1)S(1)}, bf16[192,7,128]{2,0,1:T(8,128)(2,1)}, u32[]{:S(2)}) copy-start(bf16[192,7,128]{2,0,1:T(8,128)(2,1)} %copy-done.6) | copy-start | bytes 1032196
  76.5 1.9 %copy-start.2 = (bf16[192,1,7,1536]{3,0,2,1:T(8,128)(2,1)}, bf16[192,1,7,1536]{3,0,2,1:T(8,128)(2,1)S(1)}, u32[]{:S(2)}) copy-start(bf16[192,1,7,1536]{3,0,2,1:T(8,128)(2,1)S(1)} %fusion) | copy-start | bytes 12386308
  81.0 56.3 %reduce-scatter.5.cloned.1.call-start = ((), (), s32[]{:S(2)}) async-start(), calls=%async_computation.3 | async-start | bytes 884736 | tf_op jit(solution)/shard_map/reduce_scatter | solution.py:56
  91.4 16.3 %copy-start.3 = (bf16[3584,1,128]{2,0,1:T(8,128)(2,1)S(1)}, bf16[3584,1,128]{2,0,1:T(8,128)(2,1)}, u32[]{:S(2)}) copy-start(bf16[3584,1,128]{2,0,1:T(8,128)(2,1)} %param.11) | copy-start | bytes 2752516
Sparse Core Ops, SparseCore 0:
  81.1 26.5 reduce-scatter.2
  110.8 26.5 reduce-scatter.4
where the time goes:
time: 148 us
  blocking collectives  50.2 us (34%)
  matrix products  41.2 us (28%)
  waiting for transfers between devices  31 us (21%)
  between operations  14.3 us (10%)
  local copies, waits for them, and re-layouts  6.49 us (4%)
  other arithmetic  4.3 us (3%)
    reduce_scatter x1, waiting for transfers between devices, local_layer(): dv_loc = lax.psum_scatter(dv_part, 'cp', scatter_dimension=0, tiled=True)  25.7 us
    unnamed x1, blocking collectives  25.1 us
    all_gather x1, blocking collectives, local_layer(): k_all = lax.all_gather(k_loc, 'cp', axis=0, tiled=True)  12.7 us
    all_gather x1, blocking collectives, local_layer(): v_all = lax.all_gather(v_loc, 'cp', axis=0, tiled=True)  12.4 us
    dot_general x1, matrix products, local_layer(): jnp.einsum('tkge,dkge->td', dq_loc, wq_grp, preferred_element_type=jnp.fl...  11 us
    dot_general x1, matrix products, local_layer(): jnp.einsum('tkge,kged->td', out_loc, wo_grp, preferred_element_type=jnp.f...  5.63 us
    reduce_scatter x1, waiting for transfers between devices, local_layer(): dk_loc = lax.psum_scatter(dk_part, 'cp', scatter_dimension=0, tiled=True)  5.27 us
    dot_general x1, matrix products, local_layer(): jnp.einsum('td,dkge->tkge', x_in, wq_grp, preferred_element_type=jnp.floa...  4.57 us
  transfers between devices with their start and end apart: 2, of which 2 were waited for; matrix products, arithmetic and copies ran while one was open for 17% of the time, Pallas kernels for 0%

commit v1 on v0

v1 whole, which is shorter than its diff:
```python
import functools
import math

import jax
import jax.numpy as jnp
from jax import lax
from jax.experimental import pallas as pl
from jax.experimental.pallas import tpu as pltpu
from jax.sharding import PartitionSpec as P

NEG_BIG = -1.0e30
F32 = jnp.float32
BF16 = jnp.bfloat16

NDEV = 8
HEADS = 7
E = 128
PIECE = 96
TOK = 192
D = 3584
HE = HEADS * E
ROWS = HEADS * PIECE
HALF = NDEV * PIECE
CH = 256

NT = (((1,), (1,)), ((), ()))
NN = (((1,), (0,)), ((), ()))


def dot(a, b, dims=NN):
    return lax.dot_general(a, b, dims, preferred_element_type=F32)


def kernel(x_hbm, dy_hbm, doc_ref, wq_hbm, wk_hbm, wv_hbm, wo_hbm,
           y_hbm, dx_hbm,
           x_s, dy_s, wq_s, wkv_s, wo_s,
           kv_s, doc_s, q_s, do_s, qt_s, dot_s, cap_s,
           s_s, p_s, dp_s, ds_s, o_s, dq_s, delta_s,
           accv_t, acck_t, acc_s, rb1, comb, rb2,
           y_s, dx_s, dxo_s,
           in_sem, wq_sem, wo_sem, out_sem,
           doc_send, doc_recv, kv_send, kv_recv,
           d2d_send, d2d_recv, rs_send, rs_recv):
    me = lax.axis_index('cp')
    core = lax.rem(me, 2)
    chip = me // 2
    cx = lax.rem(chip, 2)
    cy = chip // 2

    def dev(r):
        yy = lax.rem(cy + (r // 4), 2)
        xx = lax.rem(cx + ((r // 2) % 2), 2)
        cc = lax.rem(core + (r % 2), 2)
        return yy * 4 + xx * 2 + cc

    def rcopy(src, dst, ssem, rsem, r):
        return pltpu.make_async_remote_copy(src_ref=src, dst_ref=dst, send_sem=ssem, recv_sem=rsem,
                                            device_id={'cp': dev(r)}, device_id_type=pl.DeviceIdType.MESH)

    barrier = pltpu.get_barrier_semaphore()
    for r in range(1, NDEV):
        pl.semaphore_signal(barrier, inc=1, device_id={'cp': dev(r)}, device_id_type=pl.DeviceIdType.MESH)

    ld_x = pltpu.make_async_copy(x_hbm, x_s, in_sem.at[0])
    ld_wk = pltpu.make_async_copy(wk_hbm, wkv_s.at[:, 0:E], in_sem.at[1])
    ld_wv = pltpu.make_async_copy(wv_hbm, wkv_s.at[:, E:2 * E], in_sem.at[2])
    ld_dy = pltpu.make_async_copy(dy_hbm, dy_s, in_sem.at[3])
    ld_wq = [pltpu.make_async_copy(wq_hbm.at[h], wq_s.at[:, h * E:(h + 1) * E], wq_sem.at[h]) for h in range(HEADS)]
    ld_wo = [pltpu.make_async_copy(wo_hbm.at[h * E:(h + 1) * E], wo_s.at[h * E:(h + 1) * E], wo_sem.at[h])
             for h in range(HEADS)]
    for c in [ld_x, ld_wk, ld_wv] + ld_wq + [ld_dy] + ld_wo:
        c.start()

    my_off = pl.multiple_of(me * PIECE, 32)
    ld_x.wait()
    ld_wk.wait()
    ld_wv.wait()
    kv_own = dot(x_s[...], wkv_s[...]).astype(BF16)
    for t in range(2):
        for half in range(2):
            kv_s[t, half, pl.ds(my_off, PIECE), :] = kv_own[half * PIECE:(half + 1) * PIECE, t * E:(t + 1) * E]
    doc_s[me] = doc_ref[...]

    def kv_blk(owner):
        return kv_s.at[:, :, pl.ds(pl.multiple_of(owner * PIECE, 32), PIECE), :]

    pl.semaphore_wait(barrier, NDEV - 1)
    kv_out = {}
    for r in (2, 4, 6, 1):
        kv_out[r] = rcopy(kv_blk(me), kv_blk(me), kv_send.at[r], kv_recv.at[r], r)
        kv_out[r].start()
    doc_out = {}
    for r in range(1, NDEV):
        doc_out[r] = rcopy(doc_ref, doc_s.at[me], doc_send.at[r], doc_recv.at[r], r)
        doc_out[r].start()

    def kv_in(r):
        return rcopy(kv_blk(dev(r)), kv_blk(dev(r)), kv_send.at[r], kv_recv.at[r], r)

    def put_rows(dst, val, h):
        dst[0, h * PIECE:(h + 1) * PIECE, :] = val[0:PIECE]
        dst[1, h * PIECE:(h + 1) * PIECE, :] = val[PIECE:TOK]

    for h0 in range(0, HEADS, 2):
        n = min(2, HEADS - h0)
        for h in range(h0, h0 + n):
            ld_wq[h].wait()
        val = dot(x_s[...], wq_s[:, h0 * E:(h0 + n) * E]).astype(BF16)
        for j in range(n):
            put_rows(q_s, val[:, j * E:(j + 1) * E], h0 + j)

    def forward(r):
        kv_in(r).wait_recv()
        kv_out[r + 1] = rcopy(kv_blk(dev(r)), kv_blk(dev(r)), kv_send.at[r + 1], kv_recv.at[r + 1], 1)
        kv_out[r + 1].start()

    forward(2)
    forward(4)

    ld_dy.wait()
    for h0 in range(0, HEADS, 2):
        n = min(2, HEADS - h0)
        for h in range(h0, h0 + n):
            ld_wo[h].wait()
        val = dot(dy_s[...], wo_s[h0 * E:(h0 + n) * E, :], NT).astype(BF16)
        for j in range(n):
            put_rows(do_s, val[:, j * E:(j + 1) * E], h0 + j)
    forward(6)

    for piece in range(2):
        qt_s[piece] = q_s[piece].T
        dot_s[piece] = do_s[piece].T

    for r in range(1, NDEV):
        rcopy(doc_ref, doc_s.at[dev(r)], doc_send.at[r], doc_recv.at[r], r).wait_recv()
    my_doc = doc_ref[...].astype(F32)
    eye = (lax.broadcasted_iota(jnp.int32, (TOK, TOK), 0) == lax.broadcasted_iota(jnp.int32, (TOK, TOK), 1))
    doc_col = jnp.sum(jnp.where(eye, jnp.broadcast_to(my_doc, (TOK, TOK)), 0.0), axis=1, keepdims=True)
    less = jnp.zeros((TOK, TOK), F32)
    for d in range(NDEV):
        less = less + jnp.where(doc_s[d].astype(F32) < doc_col, 1.0, 0.0)
    first = jnp.sum(less, axis=1, keepdims=True)
    rowi = lax.broadcasted_iota(jnp.int32, (PIECE, 1), 0)
    pos_lo = (me * PIECE + rowi).astype(F32)
    pos_hi = ((2 * NDEV - 1 - me) * PIECE + rowi).astype(F32)
    lane = lax.broadcasted_iota(jnp.int32, (1, HALF), 1).astype(F32)
    kpos_lo = lane
    kpos_hi = (2 * NDEV - 1) * PIECE + lane - 2 * PIECE * jnp.floor((lane + 0.5) * (1.0 / PIECE))

    def cap_of(kpos, lo, hi):
        return jnp.where((kpos >= lo) & (kpos <= hi), jnp.inf, NEG_BIG)

    cap_s[:, 0:HALF] = cap_of(kpos_lo, first[PIECE:TOK], pos_hi)
    cap_s[:, HALF:2 * HALF] = cap_of(kpos_hi, first[PIECE:TOK], pos_hi)
    cap_s[:, 2 * HALF:3 * HALF] = cap_of(kpos_lo, first[0:PIECE], pos_lo)

    for r in (1, 3, 5, 7):
        kv_in(r).wait_recv()

    k_scale = E ** -0.5
    exp_scale = k_scale * math.log2(math.e)
    plan = ((1, 2, 0), (0, 1, 2))

    def key_chunks(halves):
        return [(half, c) for half in range(halves) for c in range(HALF // CH)]

    for piece, halves, col0 in plan:
        n = halves * HALF
        base = col0 * HALF
        for half, c in key_chunks(halves):
            col = base + half * HALF + c * CH
            s_s[:, col:col + CH] = dot(q_s[piece], kv_s[0, half, c * CH:(c + 1) * CH, :], NT)
        rb = 16 if halves == 2 else 32
        for h in range(HEADS):
            for b in range(PIECE // rb):
                r0 = h * PIECE + b * rb
                s = jnp.minimum(s_s[r0:r0 + rb, base:base + n], cap_s[b * rb:(b + 1) * rb, base:base + n])
                m = jnp.max(s, axis=1, keepdims=True)
                e = jnp.exp2((s - m) * exp_scale)
                l = jnp.sum(e, axis=1, keepdims=True)
                p_s[r0:r0 + rb, base:base + n] = (e * (1.0 / l)).astype(BF16)
        o = jnp.zeros((ROWS, E), F32)
        for half in range(halves):
            o = o + dot(p_s[:, base + half * HALF:base + (half + 1) * HALF], kv_s[1, half])
        o_bf = o.astype(BF16)
        delta_s[piece] = jnp.sum(do_s[piece].astype(F32) * o_bf.astype(F32), axis=1, keepdims=True)
        for h in range(HEADS):
            o_s[piece * PIECE:(piece + 1) * PIECE, h * E:(h + 1) * E] = o_bf[h * PIECE:(h + 1) * PIECE]
        for half, c in key_chunks(halves):
            col = base + half * HALF + c * CH
            dst = half * HALF + c * CH
            val = dot(dot_s[piece], p_s[:, col:col + CH])
            if piece == 0:
                val = val + accv_t[:, dst:dst + CH]
            accv_t[:, dst:dst + CH] = val

    def blk(t, owner):
        return acc_s.at[t, :, pl.ds(pl.multiple_of(owner * PIECE, 32), PIECE), :]

    def d2d(t, g):
        return rcopy(blk(t, dev(2 * g + 1)), rb1.at[t, g], d2d_send.at[t, g], d2d_recv.at[t, g], 1)

    def rs(t, g):
        return rcopy(comb.at[t, g], rb2.at[t, g], rs_send.at[t, g], rs_recv.at[t, g], 2 * g)

    def start_d2d(t, acc_t):
        for half in range(2):
            for c in range(HALF // CH):
                col = half * HALF + c * CH
                acc_s[t, half, c * CH:(c + 1) * CH, :] = acc_t[:, col:col + CH].T
        for g in (1, 2, 3, 0):
            d2d(t, g).start()

    def combine(t):
        for g in (1, 2, 3, 0):
            d2d(t, g).wait_recv()
            comb[t, g] = acc_s[t, :, pl.ds(pl.multiple_of(dev(2 * g) * PIECE, 32), PIECE), :] + rb1[t, g]
            if g:
                rs(t, g).start()

    start_d2d(1, accv_t)

    dq_parts = {}
    for piece, halves, col0 in plan:
        base = col0 * HALF
        for half, c in key_chunks(halves):
            col = base + half * HALF + c * CH
            dst = half * HALF + c * CH
            dp_s[...] = dot(do_s[piece], kv_s[1, half, c * CH:(c + 1) * CH, :], NT)
            for h in range(HEADS):
                r0 = h * PIECE
                ds_s[r0:r0 + PIECE, col:col + CH] = (
                    p_s[r0:r0 + PIECE, col:col + CH].astype(F32)
                    * (dp_s[r0:r0 + PIECE, :] - delta_s[piece, r0:r0 + PIECE, :])).astype(BF16)
            val = dot(qt_s[piece], ds_s[:, col:col + CH])
            if piece == 0:
                val = val + acck_t[:, dst:dst + CH]
            acck_t[:, dst:dst + CH] = val
        if piece == 1:
            combine(1)
        dq = jnp.zeros((ROWS, E), F32)
        for half in range(halves):
            dq = dq + dot(ds_s[:, base + half * HALF:base + (half + 1) * HALF], kv_s[0, half])
        dq_bf = (dq * k_scale).astype(BF16)
        for h in range(HEADS):
            dq_s[piece * PIECE:(piece + 1) * PIECE, h * E:(h + 1) * E] = dq_bf[h * PIECE:(h + 1) * PIECE]

    start_d2d(0, acck_t)

    NY = 512
    y_out = []
    for i in range(D // NY):
        if i == 2:
            combine(0)
        y_s[:, i * NY:(i + 1) * NY] = dot(o_s[...], wo_s[:, i * NY:(i + 1) * NY]).astype(BF16)
        cp = pltpu.make_async_copy(y_s.at[:, i * NY:(i + 1) * NY], y_hbm.at[:, i * NY:(i + 1) * NY], out_sem.at[0, i])
        cp.start()
        y_out.append(cp)
    for i in range(D // NY):
        dx_s[:, i * NY:(i + 1) * NY] = dot(dq_s[...], wq_s[i * NY:(i + 1) * NY, :], NT)

    dkv = []
    for t in range(2):
        for g in (1, 2, 3):
            rs(t, g).wait_recv()
        tot = (comb[t, 0] + rb2[t, 1]) + (rb2[t, 2] + rb2[t, 3])
        if t == 0:
            tot = tot * k_scale
        dkv.append(tot.reshape(TOK, E).astype(BF16))
    dkv = jnp.concatenate(dkv, axis=1)
    dx_out = []
    for i in range(D // NY):
        val = dx_s[:, i * NY:(i + 1) * NY] + dot(dkv, wkv_s[i * NY:(i + 1) * NY, :], NT)
        dxo_s[:, i * NY:(i + 1) * NY] = val.astype(BF16)
        cp = pltpu.make_async_copy(dxo_s.at[:, i * NY:(i + 1) * NY], dx_hbm.at[:, i * NY:(i + 1) * NY],
                                   out_sem.at[1, i])
        cp.start()
        dx_out.append(cp)

    for c in y_out + dx_out:
        c.wait()
    for r in range(1, NDEV):
        kv_out[r].wait_send()
        doc_out[r].wait_send()
    for t in range(2):
        for g in range(4):
            d2d(t, g).wait_send()
            if g:
                rs(t, g).wait_send()


def solution(mesh):
    row_spec = P(('dp', 'cp'))
    full_spec = P()
    any_spec = pl.BlockSpec(memory_space=pl.ANY)
    vmem_spec = pl.BlockSpec(memory_space=pltpu.VMEM)

    def local_layer(x_in, dy_in, doc_id, w_q, w_k, w_v, w_o):
        V = pltpu.VMEM
        dma = pltpu.SemaphoreType.DMA
        return pl.pallas_call(
            kernel,
            out_shape=(jax.ShapeDtypeStruct((TOK, D), BF16), jax.ShapeDtypeStruct((TOK, D), BF16)),
            in_specs=[any_spec, any_spec, vmem_spec, any_spec, any_spec, any_spec, any_spec],
            out_specs=(any_spec, any_spec),
            scratch_shapes=[
                V((TOK, D), BF16), V((TOK, D), BF16), V((D, HE), BF16), V((D, 2 * E), BF16), V((HE, D), BF16),
                V((2, 2, HALF, E), BF16), V((NDEV, 1, TOK), jnp.int32),
                V((2, ROWS, E), BF16), V((2, ROWS, E), BF16), V((2, E, ROWS), BF16), V((2, E, ROWS), BF16),
                V((PIECE, 3 * HALF), F32),
                V((ROWS, 3 * HALF), F32), V((ROWS, 3 * HALF), BF16), V((ROWS, CH), F32), V((ROWS, 3 * HALF), BF16),
                V((TOK, HE), BF16), V((TOK, HE), BF16), V((2, ROWS, 1), F32),
                V((E, 2 * HALF), F32), V((E, 2 * HALF), F32), V((2, 2, HALF, E), F32),
                V((2, 4, 2, PIECE, E), F32), V((2, 4, 2, PIECE, E), F32), V((2, 4, 2, PIECE, E), F32),
                V((TOK, D), BF16), V((TOK, D), F32), V((TOK, D), BF16),
                dma((4,)), dma((HEADS,)), dma((HEADS,)), dma((2, 7)),
                dma((NDEV,)), dma((NDEV,)), dma((NDEV,)), dma((NDEV,)),
                dma((2, 4)), dma((2, 4)), dma((2, 4)), dma((2, 4)),
            ],
            compiler_params=pltpu.CompilerParams(collective_id=0, has_side_effects=True,
                                                 vmem_limit_bytes=62 * 1024 * 1024),
        )(x_in, dy_in, doc_id.reshape(1, TOK), jnp.transpose(w_q, (1, 0, 2)), w_k.reshape(D, E), w_v.reshape(D, E),
          w_o.reshape(HE, D))

    return jax.shard_map(local_layer, mesh=mesh,
                         in_specs=(row_spec, row_spec, row_spec, full_spec, full_spec, full_spec, full_spec),
                         out_specs=(row_spec, row_spec), check_vma=False)
```

time: 148 us -> 43.9 us (0.30)
  blocking collectives: 50.2 us -> 0 us
  matrix products: 41.2 us -> 0 us
  Pallas kernels: 0 us -> 39.4 us
  waiting for transfers between devices: 31 us -> 0 us
  between operations: 14.3 us -> 0.65 us
  other arithmetic: 4.3 us -> 0 us
  local copies, waits for them, and re-layouts: 6.49 us -> 3.69 us
    dot_general x13 -> x0, matrix products: 41.2 us -> none  [the longest x1 11 us: local_layer(): jnp.einsum('tkge,dkge->td', dq_loc, wq_grp, preferred_element_type=jnp.fl...]
    pallas_call x0 -> x1, Pallas kernels: none -> 39.4 us  [local_layer(): pl.pallas_call(kernel, out_shape=(jax.ShapeDtypeStruct((TOK, D), BF16), j...]
    reduce_scatter x2 -> x0, waiting for transfers between devices: 31 us -> none  [the longest x1 25.7 us: local_layer(): dv_loc = lax.psum_scatter(dv_part, 'cp', scatter_dimension=0, tiled=True)]
    all_gather x2 -> x0, blocking collectives: 25.1 us -> none  [the longest x1 12.7 us: local_layer(): k_all = lax.all_gather(k_loc, 'cp', axis=0, tiled=True)]
    unnamed x1 -> x0, blocking collectives: 25.1 us -> none
    reduce_sum x1 -> x0, other arithmetic: 2.2 us -> none  [local_layer(): log_norm = jax.nn.logsumexp(scores, axis=-1, keepdims=True)]
    convert_element_type x1 -> x0, other arithmetic: 1.75 us -> none  [local_layer(): prob_bf = jnp.exp(scores - log_norm).astype(jnp.bfloat16)]
    mul x1 -> x0, local copies, waits for them, and re-layouts: 1.73 us -> none  [local_layer(): jnp.einsum('tkgs,tkge->ske', d_score, q_loc, preferred_element_type=jnp.f...]
  transfers between devices with their start and end apart: 2 -> 0, of which waited for: 2 -> 0; matrix products, arithmetic and copies ran while one was open for 17% -> 0% of each run, Pallas kernels for 0% -> 0%
where the time goes in v1:
time: 43.9 us; the launch traced here: 43.8 us
  Pallas kernels  39.4 us (90%)
  local copies, waits for them, and re-layouts  3.69 us (8%)
  between operations  0.65 us (1%)
    pallas_call x1, Pallas kernels, local_layer(): pl.pallas_call(kernel, out_shape=(jax.ShapeDtypeStruct((TOK, D), BF16), j...  39.4 us
    unnamed x4, local copies, waits for them, and re-layouts  3.69 us

profile of v1, /device:TPU:0, one launch (start us, length us, event | category | flops | bytes accessed | tf_op | source)
XLA Modules:
  0.0 43.8 jit_solution(7266568004578525287)
XLA Ops:
  0.6 39.4 %shard_map.86 = (bf16[192,3584]{1,0:T(8,128)(2,1)}, bf16[192,3584]{1,0:T(8,128)(2,1)}) custom-call(bf16[192,3584]{1,0:T(8,128)(2,1)} %x_hbm.1, bf16[192,3584]{1,0:T(8,128)(2,1)} %dy_hbm.1, s32[1,192]{1,0:T(1,128)} %bitcast.9, bf16[7,3584,128]{2,1,0:T(8,128)(2,1)} %bitcast.5, bf16[3584,128]{1,0:T(8,128)(2,1)} %bitcast.7, bf16[3584,128]{1,0:T(8,128)(2,1)} %bitcast.8, ...), custom_call_target="tpu_custom_call" | custom-call | tf_op jit(solution)/shard_map/pallas_call | solution.py:301
  40.1 0.0 copy-start
  40.1 2.6 %copy.11 = bf16[192,3584]{1,0:T(8,128)(2,1)} copy(bf16[192,3584]{1,0:T(8,128)(2,1)} %get-tuple-element.4) | data formatting | bytes 2752512
  42.7 0.0 copy-done
  42.7 1.1 %copy.12 = bf16[192,3584]{1,0:T(8,128)(2,1)} copy(bf16[192,3584]{1,0:T(8,128)(2,1)S(1)} %copy-done) | data formatting | bytes 2752512
Async XLA Ops:
  40.1 2.6 %copy-start = (bf16[192,3584]{1,0:T(8,128)(2,1)S(1)}, bf16[192,3584]{1,0:T(8,128)(2,1)}, u32[]{:S(2)}) copy-start(bf16[192,3584]{1,0:T(8,128)(2,1)} %get-tuple-element.5) | copy-start | bytes 4128772

commit v2 on v0

v2 whole, which is shorter than its diff:
```python
import math

import jax
import jax.numpy as jnp
from jax import lax
from jax.experimental import pallas as pl
from jax.experimental.pallas import tpu as pltpu
from jax.sharding import PartitionSpec as P

NEG_BIG = -1.0e30
F32 = jnp.float32
BF16 = jnp.bfloat16

NDEV = 8
HEADS = 7
E = 128
PIECE = 96
TOK = 192
D = 3584
HE = HEADS * E
ROWS = HEADS * PIECE
HALF = NDEV * PIECE
SEQ = 2 * HALF
KSPLIT = 2

NT = (((1,), (1,)), ((), ()))
NN = (((1,), (0,)), ((), ()))
UNITS = ((1, 1), (1, 0), (0, 1), (0, 0))
GROUPS = ((0, 4), (4, 7))


def dot(a, b, dims=NN):
    return lax.dot_general(a, b, dims, preferred_element_type=F32)


def main_kernel(x_hbm, dy_hbm, doc_ref, wq_hbm, wk_hbm, wv_hbm, wo_hbm,
                y_s, dx_s, dkv_s, wkv_s,
                x_s, dy_s, wq_s, wo_s,
                kv_s, doc_s, q_s, do_s, qt_s, dot_s, cap_s,
                s_s, p_s, dp_s, ds_s, o_s, dq_s, delta_s,
                acc_s, rb1, comb, rb2,
                in_sem, wq_sem, wo_sem, dy_sem,
                doc_send, doc_recv, kv_send, kv_recv,
                d2d_send, d2d_recv, rs_send, rs_recv):
    me = lax.axis_index('cp')
    core = lax.rem(me, 2)
    chip = me // 2
    cx = lax.rem(chip, 2)
    cy = chip // 2

    def dev(r):
        yy = lax.rem(cy + (r // 4), 2)
        xx = lax.rem(cx + ((r // 2) % 2), 2)
        cc = lax.rem(core + (r % 2), 2)
        return yy * 4 + xx * 2 + cc

    def rcopy(src, dst, ssem, rsem, r):
        return pltpu.make_async_remote_copy(src_ref=src, dst_ref=dst, send_sem=ssem, recv_sem=rsem,
                                            device_id={'cp': dev(r)}, device_id_type=pl.DeviceIdType.MESH)

    kd = D // KSPLIT
    ld_in = []
    for i in range(KSPLIT):
        ks = slice(i * kd, (i + 1) * kd)
        ld_in.append([pltpu.make_async_copy(x_hbm.at[:, ks], x_s.at[:, ks], in_sem.at[i, 0]),
                      pltpu.make_async_copy(wk_hbm.at[ks], wkv_s.at[ks, 0:E], in_sem.at[i, 1]),
                      pltpu.make_async_copy(wv_hbm.at[ks], wkv_s.at[ks, E:2 * E], in_sem.at[i, 2])])
    ld_dy = pltpu.make_async_copy(dy_hbm, dy_s, dy_sem)
    ld_wq = [pltpu.make_async_copy(wq_hbm.at[h], wq_s.at[:, h * E:(h + 1) * E], wq_sem.at[h]) for h in range(HEADS)]
    ld_wo = [pltpu.make_async_copy(wo_hbm.at[h * E:(h + 1) * E], wo_s.at[h * E:(h + 1) * E], wo_sem.at[h])
             for h in range(HEADS)]
    for part in ld_in:
        for c in part:
            c.start()

    barrier = pltpu.get_barrier_semaphore()
    for r in range(1, NDEV):
        pl.semaphore_signal(barrier, inc=1, device_id={'cp': dev(r)}, device_id_type=pl.DeviceIdType.MESH)

    kv_own = jnp.zeros((TOK, 2 * E), F32)
    for i in range(KSPLIT):
        for c in ld_in[i]:
            c.wait()
        if i == 0:
            for c in ld_wq[:4]:
                c.start()
        else:
            for c in ld_wq[4:]:
                c.start()
        kv_own = kv_own + dot(x_s[:, i * kd:(i + 1) * kd], wkv_s[i * kd:(i + 1) * kd, :])
    kv_own = kv_own.astype(BF16)
    my_off = pl.multiple_of(me * PIECE, 32)
    for t in range(2):
        for half in range(2):
            kv_s[t, half, pl.ds(my_off, PIECE), :] = kv_own[half * PIECE:(half + 1) * PIECE, t * E:(t + 1) * E]
    doc_s[me] = doc_ref[...]

    def kv_blk(t, owner):
        return kv_s.at[t, :, pl.ds(pl.multiple_of(owner * PIECE, 32), PIECE), :]

    pl.semaphore_wait(barrier, NDEV - 1)
    kv_out = {}
    for t in range(2):
        for r in (6, 2, 4, 1):
            kv_out[t, r] = rcopy(kv_blk(t, me), kv_blk(t, me), kv_send.at[t, r], kv_recv.at[t, r], r)
            kv_out[t, r].start()
        if t == 0:
            doc_out = {}
            for r in range(1, NDEV):
                doc_out[r] = rcopy(doc_ref, doc_s.at[me], doc_send.at[r], doc_recv.at[r], r)
                doc_out[r].start()

    def kv_in(t, r):
        return rcopy(kv_blk(t, dev(r)), kv_blk(t, dev(r)), kv_send.at[t, r], kv_recv.at[t, r], r)

    def forward(t, r):
        kv_in(t, r).wait_recv()
        kv_out[t, r + 1] = rcopy(kv_blk(t, dev(r)), kv_blk(t, dev(r)), kv_send.at[t, r + 1], kv_recv.at[t, r + 1], 1)
        kv_out[t, r + 1].start()

    def put_rows(dst, val, h):
        dst[0, h * PIECE:(h + 1) * PIECE, :] = val[0:PIECE]
        dst[1, h * PIECE:(h + 1) * PIECE, :] = val[PIECE:TOK]

    for h0, h1 in GROUPS:
        for h in range(h0, h1):
            ld_wq[h].wait()
        for c in ([ld_dy] + ld_wo[:4] if h0 == 0 else ld_wo[4:]):
            c.start()
        val = dot(x_s[...], wq_s[:, h0 * E:h1 * E]).astype(BF16)
        for h in range(h0, h1):
            put_rows(q_s, val[:, (h - h0) * E:(h - h0 + 1) * E], h)
    ld_dy.wait()
    for h0, h1 in GROUPS:
        for h in range(h0, h1):
            ld_wo[h].wait()
        val = dot(dy_s[...], wo_s[h0 * E:h1 * E, :], NT).astype(BF16)
        for h in range(h0, h1):
            put_rows(do_s, val[:, (h - h0) * E:(h - h0 + 1) * E], h)
    for r in (6, 2, 4):
        forward(0, r)

    for piece in range(2):
        qt_s[piece] = q_s[piece].T
        dot_s[piece] = do_s[piece].T

    for r in range(1, NDEV):
        rcopy(doc_ref, doc_s.at[dev(r)], doc_send.at[r], doc_recv.at[r], r).wait_recv()
    my_doc = doc_ref[...].astype(F32)
    eye = (lax.broadcasted_iota(jnp.int32, (TOK, TOK), 0) == lax.broadcasted_iota(jnp.int32, (TOK, TOK), 1))
    doc_col = jnp.sum(jnp.where(eye, jnp.broadcast_to(my_doc, (TOK, TOK)), 0.0), axis=1, keepdims=True)
    less = jnp.zeros((TOK, TOK), F32)
    for d in range(NDEV):
        less = less + jnp.where(doc_s[d].astype(F32) < doc_col, 1.0, 0.0)
    first = jnp.sum(less, axis=1, keepdims=True)
    rowi = lax.broadcasted_iota(jnp.int32, (PIECE, 1), 0)
    pos_lo = (me * PIECE + rowi).astype(F32)
    pos_hi = ((2 * NDEV - 1 - me) * PIECE + rowi).astype(F32)
    lane = lax.broadcasted_iota(jnp.int32, (1, HALF), 1).astype(F32)
    kpos_lo = lane
    kpos_hi = (2 * NDEV - 1) * PIECE + lane - 2 * PIECE * jnp.floor((lane + 0.5) * (1.0 / PIECE))

    def cap_of(kpos, lo, hi):
        return jnp.where((kpos >= lo) & (kpos <= hi), jnp.inf, NEG_BIG)

    cap_s[:, 0:HALF] = cap_of(kpos_lo, first[PIECE:TOK], pos_hi)
    cap_s[:, HALF:2 * HALF] = cap_of(kpos_hi, first[PIECE:TOK], pos_hi)
    cap_s[:, 2 * HALF:3 * HALF] = cap_of(kpos_lo, first[0:PIECE], pos_lo)

    for r in (1, 7, 3, 5):
        kv_in(0, r).wait_recv()

    k_scale = E ** -0.5
    exp_scale = k_scale * math.log2(math.e)
    plan = ((1, SEQ, 0), (0, HALF, SEQ))

    def spans(n, step=512):
        return [(h + a, h + min(a + step, HALF)) for h in range(0, n, HALF) for a in range(0, HALF, step)]

    def keys(t, a, b):
        return kv_s[t, a // HALF, a % HALF:a % HALF + (b - a), :]

    def over_keys(src, t, r0, r1, base, n):
        acc = dot(src[r0:r1, base:base + HALF], kv_s[t, 0])
        if n == SEQ:
            acc = acc + dot(src[r0:r1, base + HALF:base + SEQ], kv_s[t, 1])
        return acc

    def softmax(piece, n, base, h):
        rb = 16 if n == SEQ else 32
        for b in range(PIECE // rb):
            r0 = h * PIECE + b * rb
            s = jnp.minimum(s_s[r0:r0 + rb, base:base + n], cap_s[b * rb:(b + 1) * rb, base:base + n])
            m = jnp.max(s, axis=1, keepdims=True)
            e = jnp.exp2((s - m) * exp_scale)
            l = jnp.sum(e, axis=1, keepdims=True)
            p_s[r0:r0 + rb, base:base + n] = (e * (1.0 / l)).astype(BF16)

    def blk(t, half, owner):
        return acc_s.at[t, half, pl.ds(pl.multiple_of(owner * PIECE, 32), PIECE), :]

    def d2d(t, half, g):
        return rcopy(blk(t, half, dev(2 * g + 1)), rb1.at[t, half, g], d2d_send.at[t, half, g],
                     d2d_recv.at[t, half, g], 1)

    def rs(t, half, g):
        return rcopy(comb.at[t, half, g], rb2.at[t, half, g], rs_send.at[t, half, g], rs_recv.at[t, half, g], 2 * g)

    def start_d2d(t, half):
        for g in (3, 1, 2, 0):
            d2d(t, half, g).start()

    def combine(t, half):
        for g in (3, 1, 2, 0):
            d2d(t, half, g).wait_recv()
            comb[t, half, g] = acc_s[t, half, pl.ds(pl.multiple_of(dev(2 * g) * PIECE, 32), PIECE), :] + rb1[t, half, g]
            if g:
                rs(t, half, g).start()

    def grad(t, half, lhs_t, src):
        for a, b in spans(HALF, 256):
            val = dot(lhs_t[1], src[:, half * HALF + a:half * HALF + b])
            if half == 0:
                val = val + dot(lhs_t[0], src[:, SEQ + a:SEQ + b])
            acc_s[t, half, a:b, :] = val.T

    def s_part(piece, base, a, b):
        s_s[:, base + a:base + b] = dot(q_s[piece], keys(0, a, b), NT)

    def dp_part(piece, base, a, b):
        dp_s[:, base + a:base + b] = dot(do_s[piece], keys(1, a, b), NT)

    def o_part(piece, base, n, r0, r1):
        h0, h1 = r0 // PIECE, r1 // PIECE
        o_bf = over_keys(p_s, 1, r0, r1, base, n).astype(BF16)
        delta_s[piece, r0:r1, :] = jnp.sum(do_s[piece, r0:r1, :].astype(F32) * o_bf.astype(F32), axis=1, keepdims=True)
        for h in range(h0, h1):
            o_s[piece * PIECE:(piece + 1) * PIECE, h * E:(h + 1) * E] = o_bf[(h - h0) * PIECE:(h - h0 + 1) * PIECE]

    def ds_rows(piece, base, a, b):
        for h in range(HEADS):
            for c in range(PIECE // 32):
                r0 = h * PIECE + c * 32
                ds_s[r0:r0 + 32, base + a:base + b] = (
                    p_s[r0:r0 + 32, base + a:base + b].astype(F32)
                    * (dp_s[r0:r0 + 32, base + a:base + b] - delta_s[piece, r0:r0 + 32, :])).astype(BF16)

    def dq_part(piece, base, n):
        dq_bf = (over_keys(ds_s, 0, 0, ROWS, base, n) * k_scale).astype(BF16)
        for h in range(HEADS):
            dq_s[piece * PIECE:(piece + 1) * PIECE, h * E:(h + 1) * E] = dq_bf[h * PIECE:(h + 1) * PIECE]

    def softmax_with(piece, n, base, others):
        others = list(others)
        for h in range(HEADS):
            softmax(piece, n, base, h)
            left = HEADS - h
            take = -(-len(others) // left)
            for fn in others[:take]:
                fn()
            others = others[take:]

    for a, b in spans(SEQ):
        s_part(1, 0, a, b)
    for r in (6, 2, 4):
        forward(1, r)
    for r in (1, 7, 3, 5):
        kv_in(1, r).wait_recv()
    softmax_with(1, SEQ, 0, [lambda a=a, b=b: s_part(0, SEQ, a, b) for a, b in spans(HALF, 256)]
                 + [lambda a=a, b=b: dp_part(1, 0, a, b) for a, b in spans(SEQ, 256)])
    grad(1, 1, dot_s, p_s)
    start_d2d(1, 1)
    softmax_with(0, HALF, SEQ, [lambda: o_part(1, 0, SEQ, 0, 192), lambda: o_part(1, 0, SEQ, 192, 384),
                                lambda: o_part(1, 0, SEQ, 384, 672)]
                 + [lambda a=a, b=b: dp_part(0, SEQ, a, b) for a, b in spans(HALF, 256)])
    grad(1, 0, dot_s, p_s)
    start_d2d(1, 0)
    combine(1, 1)
    ds_rows(1, 0, HALF, SEQ)
    grad(0, 1, qt_s, ds_s)
    start_d2d(0, 1)
    o_part(0, SEQ, HALF, 0, ROWS)
    ds_rows(1, 0, 0, HALF)
    combine(1, 0)
    ds_rows(0, SEQ, 0, HALF)
    grad(0, 0, qt_s, ds_s)
    start_d2d(0, 0)
    combine(0, 1)
    for piece, n, base in plan:
        dq_part(piece, base, n)

    NY = 512

    def y_part(i):
        y_s[:, i * NY:(i + 1) * NY] = dot(o_s[...], wo_s[:, i * NY:(i + 1) * NY]).astype(BF16)

    for i in range(2):
        y_part(i)
    combine(0, 0)
    for i in range(2, D // NY):
        y_part(i)
    for i in range(D // NY):
        dx_s[:, i * NY:(i + 1) * NY] = dot(dq_s[...], wq_s[i * NY:(i + 1) * NY, :], NT)

    for t, half in UNITS:
        for g in (1, 2, 3):
            rs(t, half, g).wait_recv()
        tot = (comb[t, half, 0] + rb2[t, half, 1]) + (rb2[t, half, 2] + rb2[t, half, 3])
        if t == 0:
            tot = tot * k_scale
        dkv_s[half * PIECE:(half + 1) * PIECE, t * E:(t + 1) * E] = tot.astype(BF16)

    for r in range(1, NDEV):
        kv_out[0, r].wait_send()
        kv_out[1, r].wait_send()
        doc_out[r].wait_send()
    for t, half in UNITS:
        for g in range(4):
            d2d(t, half, g).wait_send()
            if g:
                rs(t, half, g).wait_send()


FIN = ((0, 1536), (1536, 2560), (2560, 3584))


def final_kernel(y_s, dx_s, dkv_s, wkv_s, y_hbm, dx_hbm, dxo_s, y_sem, dx_sem):
    y_cp = pltpu.make_async_copy(y_s, y_hbm, y_sem)
    y_cp.start()
    copies = [y_cp]
    for i, (a, b) in enumerate(FIN):
        dxo_s[:, a:b] = (dx_s[:, a:b] + dot(dkv_s[...], wkv_s[a:b, :], NT)).astype(BF16)
        cp = pltpu.make_async_copy(dxo_s.at[:, a:b], dx_hbm.at[:, a:b], dx_sem.at[i])
        cp.start()
        copies.append(cp)
    for cp in copies:
        cp.wait()


def solution(mesh):
    row_spec = P(('dp', 'cp'))
    full_spec = P()
    hbm_spec = pl.BlockSpec(memory_space=pltpu.HBM)
    vmem_spec = pl.BlockSpec(memory_space=pltpu.VMEM)

    def local_layer(x_in, dy_in, doc_id, w_q, w_k, w_v, w_o):
        V = pltpu.VMEM
        dma = pltpu.SemaphoreType.DMA
        sds = jax.ShapeDtypeStruct
        hbm = lambda a: pltpu.with_memory_space_constraint(a, pltpu.HBM)
        parts = pl.pallas_call(
            main_kernel,
            out_shape=(V((TOK, D), BF16), V((TOK, D), F32), V((TOK, 2 * E), BF16), V((D, 2 * E), BF16)),
            in_specs=[hbm_spec, hbm_spec, vmem_spec, hbm_spec, hbm_spec, hbm_spec, hbm_spec],
            out_specs=(vmem_spec,) * 4,
            scratch_shapes=[
                V((TOK, D), BF16), V((TOK, D), BF16), V((D, HE), BF16), V((HE, D), BF16),
                V((2, 2, HALF, E), BF16), V((NDEV, 1, TOK), jnp.int32),
                V((2, ROWS, E), BF16), V((2, ROWS, E), BF16), V((2, E, ROWS), BF16), V((2, E, ROWS), BF16),
                V((PIECE, 3 * HALF), F32),
                V((ROWS, 3 * HALF), F32), V((ROWS, 3 * HALF), BF16), V((ROWS, 3 * HALF), F32),
                V((ROWS, 3 * HALF), BF16),
                V((TOK, HE), BF16), V((TOK, HE), BF16), V((2, ROWS, 1), F32),
                V((2, 2, HALF, E), F32),
                V((2, 2, 4, PIECE, E), F32), V((2, 2, 4, PIECE, E), F32), V((2, 2, 4, PIECE, E), F32),
                dma((KSPLIT, 3)), dma((HEADS,)), dma((HEADS,)), dma,
                dma((NDEV,)), dma((NDEV,)), dma((2, NDEV)), dma((2, NDEV)),
                dma((2, 2, 4)), dma((2, 2, 4)), dma((2, 2, 4)), dma((2, 2, 4)),
            ],
            compiler_params=pltpu.CompilerParams(collective_id=0, has_side_effects=True,
                                                 vmem_limit_bytes=50 * 1024 * 1024),
        )(hbm(x_in), hbm(dy_in), doc_id.reshape(1, TOK), hbm(jnp.transpose(w_q, (1, 0, 2))), hbm(w_k.reshape(D, E)),
          hbm(w_v.reshape(D, E)), hbm(w_o.reshape(HE, D)))
        return pl.pallas_call(
            final_kernel,
            out_shape=(sds((TOK, D), BF16), sds((TOK, D), BF16)),
            in_specs=[vmem_spec] * 4,
            out_specs=(hbm_spec, hbm_spec),
            scratch_shapes=[V((TOK, D), BF16), dma, dma((len(FIN),))],
            compiler_params=pltpu.CompilerParams(vmem_limit_bytes=12 * 1024 * 1024),
        )(*[pltpu.with_memory_space_constraint(a, pltpu.VMEM) for a in parts])

    return jax.shard_map(local_layer, mesh=mesh,
                         in_specs=(row_spec, row_spec, row_spec, full_spec, full_spec, full_spec, full_spec),
                         out_specs=(row_spec, row_spec), check_vma=False)
```

time: 148 us -> 32.9 us (0.22)
  blocking collectives: 50.2 us -> 0 us
  matrix products: 41.2 us -> 0 us
  Pallas kernels: 0 us -> 32.1 us
  waiting for transfers between devices: 31 us -> 0 us
  between operations: 14.3 us -> 0.64 us
  local copies, waits for them, and re-layouts: 6.49 us -> 0 us
  other arithmetic: 4.3 us -> 0 us
    dot_general x13 -> x0, matrix products: 41.2 us -> none  [the longest x1 11 us: local_layer(): jnp.einsum('tkge,dkge->td', dq_loc, wq_grp, preferred_element_type=jnp.fl...]
    pallas_call x0 -> x2, Pallas kernels: none -> 32.1 us  [the longest x1 30.6 us: local_layer(): pl.pallas_call(main_kernel, out_shape=(V((TOK, D), BF16), V((TOK, D), F32...]
    reduce_scatter x2 -> x0, waiting for transfers between devices: 31 us -> none  [the longest x1 25.7 us: local_layer(): dv_loc = lax.psum_scatter(dv_part, 'cp', scatter_dimension=0, tiled=True)]
    all_gather x2 -> x0, blocking collectives: 25.1 us -> none  [the longest x1 12.7 us: local_layer(): k_all = lax.all_gather(k_loc, 'cp', axis=0, tiled=True)]
    unnamed x1 -> x0, blocking collectives: 25.1 us -> none
    unnamed x27 -> x0, local copies, waits for them, and re-layouts: 2.95 us -> none
    reduce_sum x1 -> x0, other arithmetic: 2.2 us -> none  [local_layer(): log_norm = jax.nn.logsumexp(scores, axis=-1, keepdims=True)]
    convert_element_type x1 -> x0, other arithmetic: 1.75 us -> none  [local_layer(): prob_bf = jnp.exp(scores - log_norm).astype(jnp.bfloat16)]
  transfers between devices with their start and end apart: 2 -> 0, of which waited for: 2 -> 0; matrix products, arithmetic and copies ran while one was open for 17% -> 0% of each run, Pallas kernels for 0% -> 0%
where the time goes in v2:
time: 32.9 us; the launch traced here: 32.8 us
  Pallas kernels  32.1 us (98%)
  between operations  0.64 us (2%)
    pallas_call x1, Pallas kernels, local_layer(): pl.pallas_call(main_kernel, out_shape=(V((TOK, D), BF16), V((TOK, D), F32...  30.6 us
    pallas_call x1, Pallas kernels, local_layer(): pl.pallas_call(final_kernel, out_shape=(sds((TOK, D), BF16), sds((TOK, D)...  1.57 us

profile of v2, /device:TPU:0, one launch (start us, length us, event | category | flops | bytes accessed | tf_op | source)
XLA Modules:
  0.0 32.8 jit_solution(6424141737432024781)
XLA Ops:
  0.6 30.6 %shard_map.86 = (bf16[192,3584]{1,0:T(8,128)(2,1)S(1)}, f32[192,3584]{1,0:T(8,128)S(1)}, bf16[192,256]{1,0:T(8,128)(2,1)S(1)}, bf16[3584,256]{1,0:T(8,128)(2,1)S(1)}) custom-call(bf16[192,3584]{1,0:T(8,128)(2,1)} %x_hbm.1, bf16[192,3584]{1,0:T(8,128)(2,1)} %dy_hbm.1, s32[1,192]{1,0:T(1,128)} %bitcast.9, bf16[7,3584,128]{2,1,0:T(8,128)(2,1)} %bitcast.5, ...), custom_call_target="tpu_custom_call" | custom-call | tf_op jit(solution)/shard_map/pallas_call | solution.py:351
  31.2 1.6 %shard_map.87 = (bf16[192,3584]{1,0:T(8,128)(2,1)}, bf16[192,3584]{1,0:T(8,128)(2,1)}) custom-call(bf16[192,3584]{1,0:T(8,128)(2,1)S(1)} %get-tuple-element.6.y_s, f32[192,3584]{1,0:T(8,128)S(1)} %get-tuple-element.7.dx_s, bf16[192,256]{1,0:T(8,128)(2,1)S(1)} %get-tuple-element.8.dkv_s, bf16[3584,256]{1,0:T(8,128)(2,1)S(1)} %get-tuple-element.9.wkv_s), custom_call_target="tpu_custom_call" | custom-call | tf_op jit(solution)/shard_map/pallas_call | solution.py:374

commit v3 on v2

--- a/solution.py
+++ b/solution.py
@@ -31,6 +31,10 @@
 
 def dot(a, b, dims=NN):
     return lax.dot_general(a, b, dims, preferred_element_type=F32)
+
+
+def side_by_side(ref, h0, h1, r0, r1):
+    return jnp.concatenate([ref[h, r0:r1, :] for h in range(h0, h1)], axis=1)
 
 
 def main_kernel(x_hbm, dy_hbm, doc_ref, wq_hbm, wk_hbm, wv_hbm, wo_hbm,
@@ -63,52 +67,49 @@
     for i in range(KSPLIT):
         ks = slice(i * kd, (i + 1) * kd)
         ld_in.append([pltpu.make_async_copy(x_hbm.at[:, ks], x_s.at[:, ks], in_sem.at[i, 0]),
-                      pltpu.make_async_copy(wk_hbm.at[ks], wkv_s.at[ks, 0:E], in_sem.at[i, 1]),
-                      pltpu.make_async_copy(wv_hbm.at[ks], wkv_s.at[ks, E:2 * E], in_sem.at[i, 2])])
+                      pltpu.make_async_copy(wk_hbm.at[ks], wkv_s.at[0, ks], in_sem.at[i, 1]),
+                      pltpu.make_async_copy(wv_hbm.at[ks], wkv_s.at[1, ks], in_sem.at[i, 2])])
     ld_dy = pltpu.make_async_copy(dy_hbm, dy_s, dy_sem)
-    ld_wq = [pltpu.make_async_copy(wq_hbm.at[h], wq_s.at[:, h * E:(h + 1) * E], wq_sem.at[h]) for h in range(HEADS)]
+    ld_wq = [pltpu.make_async_copy(wq_hbm.at[h], wq_s.at[h], wq_sem.at[h]) for h in range(HEADS)]
     ld_wo = [pltpu.make_async_copy(wo_hbm.at[h * E:(h + 1) * E], wo_s.at[h * E:(h + 1) * E], wo_sem.at[h])
              for h in range(HEADS)]
-    for part in ld_in:
+    for part in ld_in + [ld_wq[:1]]:
         for c in part:
             c.start()
+    LATER = (ld_wq[1:], [ld_dy] + ld_wo[:4])
 
     barrier = pltpu.get_barrier_semaphore()
     for r in range(1, NDEV):
         pl.semaphore_signal(barrier, inc=1, device_id={'cp': dev(r)}, device_id_type=pl.DeviceIdType.MESH)
 
-    kv_own = jnp.zeros((TOK, 2 * E), F32)
     for i in range(KSPLIT):
         for c in ld_in[i]:
             c.wait()
+        for c in LATER[i]:
+            c.start()
+        kv_part = dot(x_s[:, i * kd:(i + 1) * kd], side_by_side(wkv_s, 0, 2, i * kd, (i + 1) * kd))
         if i == 0:
-            for c in ld_wq[:4]:
-                c.start()
-        else:
-            for c in ld_wq[4:]:
-                c.start()
-        kv_own = kv_own + dot(x_s[:, i * kd:(i + 1) * kd], wkv_s[i * kd:(i + 1) * kd, :])
-    kv_own = kv_own.astype(BF16)
+            s_s[0:TOK, 0:2 * E] = kv_part
+            pl.semaphore_wait(barrier, NDEV - 1)
+            doc_s[me] = doc_ref[...]
+            doc_out = {}
+            for r in range(1, NDEV):
+                doc_out[r] = rcopy(doc_ref, doc_s.at[me], doc_send.at[r], doc_recv.at[r], r)
+                doc_out[r].start()
+    kv_own = (s_s[0:TOK, 0:2 * E] + kv_part).astype(BF16)
     my_off = pl.multiple_of(me * PIECE, 32)
     for t in range(2):
         for half in range(2):
             kv_s[t, half, pl.ds(my_off, PIECE), :] = kv_own[half * PIECE:(half + 1) * PIECE, t * E:(t + 1) * E]
-    doc_s[me] = doc_ref[...]
 
     def kv_blk(t, owner):
         return kv_s.at[t, :, pl.ds(pl.multiple_of(owner * PIECE, 32), PIECE), :]
 
-    pl.semaphore_wait(barrier, NDEV - 1)
     kv_out = {}
     for t in range(2):
         for r in (6, 2, 4, 1):
             kv_out[t, r] = rcopy(kv_blk(t, me), kv_blk(t, me), kv_send.at[t, r], kv_recv.at[t, r], r)
             kv_out[t, r].start()
-        if t == 0:
-            doc_out = {}
-            for r in range(1, NDEV):
-                doc_out[r] = rcopy(doc_ref, doc_s.at[me], doc_send.at[r], doc_recv.at[r], r)
-                doc_out[r].start()
 
     def kv_in(t, r):
         return rcopy(kv_blk(t, dev(r)), kv_blk(t, dev(r)), kv_send.at[t, r], kv_recv.at[t, r], r)
@@ -125,25 +126,11 @@
     for h0, h1 in GROUPS:
         for h in range(h0, h1):
             ld_wq[h].wait()
-        for c in ([ld_dy] + ld_wo[:4] if h0 == 0 else ld_wo[4:]):
+        for c in (ld_wo[4:] if h0 == 0 else []):
             c.start()
-        val = dot(x_s[...], wq_s[:, h0 * E:h1 * E]).astype(BF16)
+        val = dot(x_s[...], side_by_side(wq_s, h0, h1, 0, D)).astype(BF16)
         for h in range(h0, h1):
             put_rows(q_s, val[:, (h - h0) * E:(h - h0 + 1) * E], h)
-    ld_dy.wait()
-    for h0, h1 in GROUPS:
-        for h in range(h0, h1):
-            ld_wo[h].wait()
-        val = dot(dy_s[...], wo_s[h0 * E:h1 * E, :], NT).astype(BF16)
-        for h in range(h0, h1):
-            put_rows(do_s, val[:, (h - h0) * E:(h - h0 + 1) * E], h)
-    for r in (6, 2, 4):
-        forward(0, r)
-
-    for piece in range(2):
-        qt_s[piece] = q_s[piece].T
-        dot_s[piece] = do_s[piece].T
-
     for r in range(1, NDEV):
         rcopy(doc_ref, doc_s.at[dev(r)], doc_send.at[r], doc_recv.at[r], r).wait_recv()
     my_doc = doc_ref[...].astype(F32)
@@ -167,6 +154,20 @@
     cap_s[:, HALF:2 * HALF] = cap_of(kpos_hi, first[PIECE:TOK], pos_hi)
     cap_s[:, 2 * HALF:3 * HALF] = cap_of(kpos_lo, first[0:PIECE], pos_lo)
 
+    ld_dy.wait()
+    for h0, h1 in GROUPS:
+        for h in range(h0, h1):
+            ld_wo[h].wait()
+        val = dot(dy_s[...], wo_s[h0 * E:h1 * E, :], NT).astype(BF16)
+        for h in range(h0, h1):
+            put_rows(do_s, val[:, (h - h0) * E:(h - h0 + 1) * E], h)
+    for r in (6, 2, 4):
+        forward(0, r)
+
+    for piece in range(2):
+        qt_s[piece] = q_s[piece].T
+        dot_s[piece] = do_s[piece].T
+
     for r in (1, 7, 3, 5):
         kv_in(0, r).wait_recv()
 
@@ -181,10 +182,13 @@
         return kv_s[t, a // HALF, a % HALF:a % HALF + (b - a), :]
 
     def over_keys(src, t, r0, r1, base, n):
-        acc = dot(src[r0:r1, base:base + HALF], kv_s[t, 0])
-        if n == SEQ:
-            acc = acc + dot(src[r0:r1, base + HALF:base + SEQ], kv_s[t, 1])
-        return acc
+        parts = []
+        for a, b in ((r0, (r0 + r1) // 2), ((r0 + r1) // 2, r1)):
+            acc = dot(src[a:b, base:base + HALF], kv_s[t, 0])
+            if n == SEQ:
+                acc = acc + dot(src[a:b, base + HALF:base + SEQ], kv_s[t, 1])
+            parts.append(acc)
+        return jnp.concatenate(parts, axis=0)
 
     def softmax(piece, n, base, h):
         rb = 16 if n == SEQ else 32
@@ -250,11 +254,10 @@
         for h in range(HEADS):
             dq_s[piece * PIECE:(piece + 1) * PIECE, h * E:(h + 1) * E] = dq_bf[h * PIECE:(h + 1) * PIECE]
 
-    def softmax_with(piece, n, base, others):
-        others = list(others)
-        for h in range(HEADS):
+    def softmax_with(piece, n, base, h0, h1, others):
+        for h in range(h0, h1):
             softmax(piece, n, base, h)
-            left = HEADS - h
+            left = h1 - h
             take = -(-len(others) // left)
             for fn in others[:take]:
                 fn()
@@ -262,26 +265,27 @@
 
     for a, b in spans(SEQ):
         s_part(1, 0, a, b)
+    softmax_with(1, SEQ, 0, 0, 4, [lambda a=a, b=b: s_part(0, SEQ, a, b) for a, b in spans(HALF, 256)])
     for r in (6, 2, 4):
         forward(1, r)
+    softmax_with(1, SEQ, 0, 4, HEADS, [])
+    grad(1, 1, dot_s, p_s)
+    start_d2d(1, 1)
     for r in (1, 7, 3, 5):
         kv_in(1, r).wait_recv()
-    softmax_with(1, SEQ, 0, [lambda a=a, b=b: s_part(0, SEQ, a, b) for a, b in spans(HALF, 256)]
-                 + [lambda a=a, b=b: dp_part(1, 0, a, b) for a, b in spans(SEQ, 256)])
-    grad(1, 1, dot_s, p_s)
-    start_d2d(1, 1)
-    softmax_with(0, HALF, SEQ, [lambda: o_part(1, 0, SEQ, 0, 192), lambda: o_part(1, 0, SEQ, 192, 384),
-                                lambda: o_part(1, 0, SEQ, 384, 672)]
-                 + [lambda a=a, b=b: dp_part(0, SEQ, a, b) for a, b in spans(HALF, 256)])
+    softmax_with(0, HALF, SEQ, 0, HEADS, [lambda a=a, b=b: dp_part(1, 0, a, b) for a, b in spans(SEQ, 256)])
+    combine(1, 1)
     grad(1, 0, dot_s, p_s)
     start_d2d(1, 0)
-    combine(1, 1)
+    o_part(1, 0, SEQ, 0, ROWS)
     ds_rows(1, 0, HALF, SEQ)
+    for a, b in spans(HALF):
+        dp_part(0, SEQ, a, b)
     grad(0, 1, qt_s, ds_s)
     start_d2d(0, 1)
+    combine(1, 0)
     o_part(0, SEQ, HALF, 0, ROWS)
     ds_rows(1, 0, 0, HALF)
-    combine(1, 0)
     ds_rows(0, SEQ, 0, HALF)
     grad(0, 0, qt_s, ds_s)
     start_d2d(0, 0)
@@ -289,7 +293,7 @@
     for piece, n, base in plan:
         dq_part(piece, base, n)
 
-    NY = 512
+    NY = 896
 
     def y_part(i):
         y_s[:, i * NY:(i + 1) * NY] = dot(o_s[...], wo_s[:, i * NY:(i + 1) * NY]).astype(BF16)
@@ -300,7 +304,7 @@
     for i in range(2, D // NY):
         y_part(i)
     for i in range(D // NY):
-        dx_s[:, i * NY:(i + 1) * NY] = dot(dq_s[...], wq_s[i * NY:(i + 1) * NY, :], NT)
+        dx_s[:, i * NY:(i + 1) * NY] = dot(dq_s[...], side_by_side(wq_s, 0, HEADS, i * NY, (i + 1) * NY), NT)
 
     for t, half in UNITS:
         for g in (1, 2, 3):
@@ -329,7 +333,7 @@
     y_cp.start()
     copies = [y_cp]
     for i, (a, b) in enumerate(FIN):
-        dxo_s[:, a:b] = (dx_s[:, a:b] + dot(dkv_s[...], wkv_s[a:b, :], NT)).astype(BF16)
+        dxo_s[:, a:b] = (dx_s[:, a:b] + dot(dkv_s[...], side_by_side(wkv_s, 0, 2, a, b), NT)).astype(BF16)
         cp = pltpu.make_async_copy(dxo_s.at[:, a:b], dx_hbm.at[:, a:b], dx_sem.at[i])
         cp.start()
         copies.append(cp)
@@ -350,11 +354,11 @@
         hbm = lambda a: pltpu.with_memory_space_constraint(a, pltpu.HBM)
         parts = pl.pallas_call(
             main_kernel,
-            out_shape=(V((TOK, D), BF16), V((TOK, D), F32), V((TOK, 2 * E), BF16), V((D, 2 * E), BF16)),
+            out_shape=(V((TOK, D), BF16), V((TOK, D), F32), V((TOK, 2 * E), BF16), V((2, D, E), BF16)),
             in_specs=[hbm_spec, hbm_spec, vmem_spec, hbm_spec, hbm_spec, hbm_spec, hbm_spec],
             out_specs=(vmem_spec,) * 4,
             scratch_shapes=[
-                V((TOK, D), BF16), V((TOK, D), BF16), V((D, HE), BF16), V((HE, D), BF16),
+                V((TOK, D), BF16), V((TOK, D), BF16), V((HEADS, D, E), BF16), V((HE, D), BF16),
                 V((2, 2, HALF, E), BF16), V((NDEV, 1, TOK), jnp.int32),
                 V((2, ROWS, E), BF16), V((2, ROWS, E), BF16), V((2, E, ROWS), BF16), V((2, E, ROWS), BF16),
                 V((PIECE, 3 * HALF), F32),

time: 32.9 us -> 30.5 us (0.927)
  Pallas kernels: 32.1 us -> 29.7 us
    pallas_call x1, Pallas kernels: 30.6 us -> 28.2 us  [local_layer(): pl.pallas_call(main_kernel, out_shape=(V((TOK, D), BF16), V((TOK, D), F32...]
where the time goes in v3:
time: 30.5 us; the launch traced here: 30.4 us
  Pallas kernels  29.7 us (97%)
  between operations  0.64 us (2%)
    pallas_call x1, Pallas kernels, local_layer(): pl.pallas_call(main_kernel, out_shape=(V((TOK, D), BF16), V((TOK, D), F32...  28.2 us
    pallas_call x1, Pallas kernels, local_layer(): pl.pallas_call(final_kernel, out_shape=(sds((TOK, D), BF16), sds((TOK, D)...  1.56 us

profile of v3, /device:TPU:0, one launch (start us, length us, event | category | flops | bytes accessed | tf_op | source)
XLA Modules:
  0.0 30.4 jit_solution(2954394103871166681)
XLA Ops:
  0.6 28.2 %shard_map.86 = (bf16[192,3584]{1,0:T(8,128)(2,1)S(1)}, f32[192,3584]{1,0:T(8,128)S(1)}, bf16[192,256]{1,0:T(8,128)(2,1)S(1)}, bf16[2,3584,128]{2,1,0:T(8,128)(2,1)S(1)}) custom-call(bf16[192,3584]{1,0:T(8,128)(2,1)} %x_hbm.1, bf16[192,3584]{1,0:T(8,128)(2,1)} %dy_hbm.1, s32[1,192]{1,0:T(1,128)} %bitcast.9, bf16[7,3584,128]{2,1,0:T(8,128)(2,1)} %bitcast.5, ...), custom_call_target="tpu_custom_call" | custom-call | tf_op jit(solution)/shard_map/pallas_call | solution.py:355
  28.8 1.6 %shard_map.87 = (bf16[192,3584]{1,0:T(8,128)(2,1)}, bf16[192,3584]{1,0:T(8,128)(2,1)}) custom-call(bf16[192,3584]{1,0:T(8,128)(2,1)S(1)} %get-tuple-element.6.y_s, f32[192,3584]{1,0:T(8,128)S(1)} %get-tuple-element.7.dx_s, bf16[192,256]{1,0:T(8,128)(2,1)S(1)} %get-tuple-element.8.dkv_s, bf16[2,3584,128]{2,1,0:T(8,128)(2,1)S(1)} %get-tuple-element.9.wkv_s), custom_call_target="tpu_custom_call" | custom-call | tf_op jit(solution)/shard_map/pallas_call | solution.py:378

commit v4 on v3

--- a/solution.py
+++ b/solution.py
@@ -21,7 +21,7 @@
 ROWS = HEADS * PIECE
 HALF = NDEV * PIECE
 SEQ = 2 * HALF
-KSPLIT = 2
+KPARTS = ((0, 1024), (1024, 2048), (2048, 3072), (3072, D))
 
 NT = (((1,), (1,)), ((), ()))
 NN = (((1,), (0,)), ((), ()))
@@ -42,7 +42,7 @@
                 x_s, dy_s, wq_s, wo_s,
                 kv_s, doc_s, q_s, do_s, qt_s, dot_s, cap_s,
                 s_s, p_s, dp_s, ds_s, o_s, dq_s, delta_s,
-                acc_s, rb1, comb, rb2,
+                acc_s, rb1, comb, rb2, relay,
                 in_sem, wq_sem, wo_sem, dy_sem,
                 doc_send, doc_recv, kv_send, kv_recv,
                 d2d_send, d2d_recv, rs_send, rs_recv):
@@ -62,10 +62,9 @@
         return pltpu.make_async_remote_copy(src_ref=src, dst_ref=dst, send_sem=ssem, recv_sem=rsem,
                                             device_id={'cp': dev(r)}, device_id_type=pl.DeviceIdType.MESH)
 
-    kd = D // KSPLIT
     ld_in = []
-    for i in range(KSPLIT):
-        ks = slice(i * kd, (i + 1) * kd)
+    for i, (ka, kb) in enumerate(KPARTS):
+        ks = slice(ka, kb)
         ld_in.append([pltpu.make_async_copy(x_hbm.at[:, ks], x_s.at[:, ks], in_sem.at[i, 0]),
                       pltpu.make_async_copy(wk_hbm.at[ks], wkv_s.at[0, ks], in_sem.at[i, 1]),
                       pltpu.make_async_copy(wv_hbm.at[ks], wkv_s.at[1, ks], in_sem.at[i, 2])])
@@ -76,27 +75,30 @@
     for part in ld_in + [ld_wq[:1]]:
         for c in part:
             c.start()
-    LATER = (ld_wq[1:], [ld_dy] + ld_wo[:4])
+    LATER = (ld_wq[1:3], ld_wq[3:4], ld_wq[4:], [])
 
     barrier = pltpu.get_barrier_semaphore()
     for r in range(1, NDEV):
         pl.semaphore_signal(barrier, inc=1, device_id={'cp': dev(r)}, device_id_type=pl.DeviceIdType.MESH)
 
-    for i in range(KSPLIT):
+    for i, (ka, kb) in enumerate(KPARTS):
         for c in ld_in[i]:
             c.wait()
         for c in LATER[i]:
             c.start()
-        kv_part = dot(x_s[:, i * kd:(i + 1) * kd], side_by_side(wkv_s, 0, 2, i * kd, (i + 1) * kd))
-        if i == 0:
+        kv_part = dot(x_s[:, ka:kb], side_by_side(wkv_s, 0, 2, ka, kb))
+        if i:
+            kv_part = s_s[0:TOK, 0:2 * E] + kv_part
+        if i < len(KPARTS) - 1:
             s_s[0:TOK, 0:2 * E] = kv_part
+        if i == 1:
             pl.semaphore_wait(barrier, NDEV - 1)
             doc_s[me] = doc_ref[...]
             doc_out = {}
             for r in range(1, NDEV):
                 doc_out[r] = rcopy(doc_ref, doc_s.at[me], doc_send.at[r], doc_recv.at[r], r)
                 doc_out[r].start()
-    kv_own = (s_s[0:TOK, 0:2 * E] + kv_part).astype(BF16)
+    kv_own = kv_part.astype(BF16)
     my_off = pl.multiple_of(me * PIECE, 32)
     for t in range(2):
         for half in range(2):
@@ -126,34 +128,13 @@
     for h0, h1 in GROUPS:
         for h in range(h0, h1):
             ld_wq[h].wait()
-        for c in (ld_wo[4:] if h0 == 0 else []):
+        for c in ([ld_dy] + ld_wo[:4] if h0 == 0 else ld_wo[4:]):
             c.start()
         val = dot(x_s[...], side_by_side(wq_s, h0, h1, 0, D)).astype(BF16)
         for h in range(h0, h1):
             put_rows(q_s, val[:, (h - h0) * E:(h - h0 + 1) * E], h)
     for r in range(1, NDEV):
         rcopy(doc_ref, doc_s.at[dev(r)], doc_send.at[r], doc_recv.at[r], r).wait_recv()
-    my_doc = doc_ref[...].astype(F32)
-    eye = (lax.broadcasted_iota(jnp.int32, (TOK, TOK), 0) == lax.broadcasted_iota(jnp.int32, (TOK, TOK), 1))
-    doc_col = jnp.sum(jnp.where(eye, jnp.broadcast_to(my_doc, (TOK, TOK)), 0.0), axis=1, keepdims=True)
-    less = jnp.zeros((TOK, TOK), F32)
-    for d in range(NDEV):
-        less = less + jnp.where(doc_s[d].astype(F32) < doc_col, 1.0, 0.0)
-    first = jnp.sum(less, axis=1, keepdims=True)
-    rowi = lax.broadcasted_iota(jnp.int32, (PIECE, 1), 0)
-    pos_lo = (me * PIECE + rowi).astype(F32)
-    pos_hi = ((2 * NDEV - 1 - me) * PIECE + rowi).astype(F32)
-    lane = lax.broadcasted_iota(jnp.int32, (1, HALF), 1).astype(F32)
-    kpos_lo = lane
-    kpos_hi = (2 * NDEV - 1) * PIECE + lane - 2 * PIECE * jnp.floor((lane + 0.5) * (1.0 / PIECE))
-
-    def cap_of(kpos, lo, hi):
-        return jnp.where((kpos >= lo) & (kpos <= hi), jnp.inf, NEG_BIG)
-
-    cap_s[:, 0:HALF] = cap_of(kpos_lo, first[PIECE:TOK], pos_hi)
-    cap_s[:, HALF:2 * HALF] = cap_of(kpos_hi, first[PIECE:TOK], pos_hi)
-    cap_s[:, 2 * HALF:3 * HALF] = cap_of(kpos_lo, first[0:PIECE], pos_lo)
-
     ld_dy.wait()
     for h0, h1 in GROUPS:
         for h in range(h0, h1):
@@ -161,12 +142,32 @@
         val = dot(dy_s[...], wo_s[h0 * E:h1 * E, :], NT).astype(BF16)
         for h in range(h0, h1):
             put_rows(do_s, val[:, (h - h0) * E:(h - h0 + 1) * E], h)
-    for r in (6, 2, 4):
-        forward(0, r)
-
-    for piece in range(2):
-        qt_s[piece] = q_s[piece].T
-        dot_s[piece] = do_s[piece].T
+        if h0 == 0:
+            my_doc = doc_ref[...].astype(F32)
+            eye = (lax.broadcasted_iota(jnp.int32, (TOK, TOK), 0) == lax.broadcasted_iota(jnp.int32, (TOK, TOK), 1))
+            doc_col = jnp.sum(jnp.where(eye, jnp.broadcast_to(my_doc, (TOK, TOK)), 0.0), axis=1, keepdims=True)
+            less = jnp.zeros((TOK, TOK), F32)
+            for d in range(NDEV):
+                less = less + jnp.where(doc_s[d].astype(F32) < doc_col, 1.0, 0.0)
+            first = jnp.sum(less, axis=1, keepdims=True)
+            rowi = lax.broadcasted_iota(jnp.int32, (PIECE, 1), 0)
+            pos_lo = (me * PIECE + rowi).astype(F32)
+            pos_hi = ((2 * NDEV - 1 - me) * PIECE + rowi).astype(F32)
+            lane = lax.broadcasted_iota(jnp.int32, (1, HALF), 1).astype(F32)
+            kpos_lo = lane
+            kpos_hi = (2 * NDEV - 1) * PIECE + lane - 2 * PIECE * jnp.floor((lane + 0.5) * (1.0 / PIECE))
+
+            def cap_of(kpos, lo, hi):
+                return jnp.where((kpos >= lo) & (kpos <= hi), jnp.inf, NEG_BIG)
+
+            cap_s[:, 0:HALF] = cap_of(kpos_lo, first[PIECE:TOK], pos_hi)
+            cap_s[:, HALF:2 * HALF] = cap_of(kpos_hi, first[PIECE:TOK], pos_hi)
+            cap_s[:, 2 * HALF:3 * HALF] = cap_of(kpos_lo, first[0:PIECE], pos_lo)
+            for r in (6, 2, 4):
+                forward(0, r)
+        else:
+            for piece in range(2):
+                qt_s[piece] = q_s[piece].T
 
     for r in (1, 7, 3, 5):
         kv_in(0, r).wait_recv()
@@ -214,12 +215,47 @@
         for g in (3, 1, 2, 0):
             d2d(t, half, g).start()
 
-    def combine(t, half):
+    def add_peer(t, half, g):
+        d2d(t, half, g).wait_recv()
+        comb[t, half, g] = (acc_s[t, half, pl.ds(pl.multiple_of(dev(2 * g) * PIECE, 32), PIECE), :]
+                            + rb1[t, half, g])
+
+    def combine_direct(t, half):
         for g in (3, 1, 2, 0):
-            d2d(t, half, g).wait_recv()
-            comb[t, half, g] = acc_s[t, half, pl.ds(pl.multiple_of(dev(2 * g) * PIECE, 32), PIECE), :] + rb1[t, half, g]
+            add_peer(t, half, g)
             if g:
                 rs(t, half, g).start()
+
+    first_dev = lax.rem(cy + core, 2) * 4 + lax.rem(cx + 1 - core, 2) * 2 + core
+    second_dev = lax.rem(cy + 1 - core, 2) * 4 + lax.rem(cx + core, 2) * 2 + core
+    first_g, second_g = 1 + core, 2 - core
+
+    def to_first(t, half, i):
+        if i == 0:
+            src, dst = comb.at[t, half, 3], relay.at[t, half]
+        else:
+            src, dst = comb.at[t, half, first_g], rb2.at[t, half, 1]
+        return pltpu.make_async_remote_copy(
+            src_ref=src, dst_ref=dst, send_sem=rs_send.at[t, half, i], recv_sem=rs_recv.at[t, half, i],
+            device_id={'cp': first_dev}, device_id_type=pl.DeviceIdType.MESH)
+
+    def to_second(t, half):
+        return pltpu.make_async_remote_copy(
+            src_ref=comb.at[t, half, second_g], dst_ref=rb2.at[t, half, 2], send_sem=rs_send.at[t, half, 2],
+            recv_sem=rs_recv.at[t, half, 2], device_id={'cp': second_dev}, device_id_type=pl.DeviceIdType.MESH)
+
+    def combine_relayed(t, half):
+        add_peer(t, half, 3)
+        to_first(t, half, 0).start()
+        add_peer(t, half, 1)
+        add_peer(t, half, 2)
+        to_first(t, half, 1).start()
+        add_peer(t, half, 0)
+
+    def pass_on(t, half):
+        to_first(t, half, 0).wait_recv()
+        comb[t, half, second_g] = comb[t, half, second_g] + relay[t, half]
+        to_second(t, half).start()
 
     def grad(t, half, lhs_t, src):
         for a, b in spans(HALF, 256):
@@ -265,6 +301,8 @@
 
     for a, b in spans(SEQ):
         s_part(1, 0, a, b)
+    for piece in range(2):
+        dot_s[piece] = do_s[piece].T
     softmax_with(1, SEQ, 0, 0, 4, [lambda a=a, b=b: s_part(0, SEQ, a, b) for a, b in spans(HALF, 256)])
     for r in (6, 2, 4):
         forward(1, r)
@@ -274,7 +312,7 @@
     for r in (1, 7, 3, 5):
         kv_in(1, r).wait_recv()
     softmax_with(0, HALF, SEQ, 0, HEADS, [lambda a=a, b=b: dp_part(1, 0, a, b) for a, b in spans(SEQ, 256)])
-    combine(1, 1)
+    combine_relayed(1, 1)
     grad(1, 0, dot_s, p_s)
     start_d2d(1, 0)
     o_part(1, 0, SEQ, 0, ROWS)
@@ -283,36 +321,42 @@
         dp_part(0, SEQ, a, b)
     grad(0, 1, qt_s, ds_s)
     start_d2d(0, 1)
-    combine(1, 0)
+    combine_relayed(1, 0)
     o_part(0, SEQ, HALF, 0, ROWS)
     ds_rows(1, 0, 0, HALF)
     ds_rows(0, SEQ, 0, HALF)
     grad(0, 0, qt_s, ds_s)
     start_d2d(0, 0)
-    combine(0, 1)
+    pass_on(1, 1)
+    combine_relayed(0, 1)
     for piece, n, base in plan:
         dq_part(piece, base, n)
 
+    combine_direct(0, 0)
     NY = 896
 
-    def y_part(i):
-        y_s[:, i * NY:(i + 1) * NY] = dot(o_s[...], wo_s[:, i * NY:(i + 1) * NY]).astype(BF16)
-
-    for i in range(2):
-        y_part(i)
-    combine(0, 0)
-    for i in range(2, D // NY):
-        y_part(i)
+    def y_part(a, b):
+        y_s[:, a:b] = dot(o_s[...], wo_s[:, a:b]).astype(BF16)
+
+    y_part(0, 1792)
+    pass_on(1, 0)
+    y_part(1792, D)
+    pass_on(0, 1)
     for i in range(D // NY):
         dx_s[:, i * NY:(i + 1) * NY] = dot(dq_s[...], side_by_side(wq_s, 0, HEADS, i * NY, (i + 1) * NY), NT)
 
-    for t, half in UNITS:
-        for g in (1, 2, 3):
-            rs(t, half, g).wait_recv()
-        tot = (comb[t, half, 0] + rb2[t, half, 1]) + (rb2[t, half, 2] + rb2[t, half, 3])
+    def put_total(t, half, tot):
         if t == 0:
             tot = tot * k_scale
         dkv_s[half * PIECE:(half + 1) * PIECE, t * E:(t + 1) * E] = tot.astype(BF16)
+
+    for t, half in UNITS[:3]:
+        to_first(t, half, 1).wait_recv()
+        to_second(t, half).wait_recv()
+        put_total(t, half, comb[t, half, 0] + (rb2[t, half, 1] + rb2[t, half, 2]))
+    for g in (3, 1, 2):
+        rs(0, 0, g).wait_recv()
+    put_total(0, 0, (comb[0, 0, 0] + rb2[0, 0, 1]) + (rb2[0, 0, 2] + rb2[0, 0, 3]))
 
     for r in range(1, NDEV):
         kv_out[0, r].wait_send()
@@ -321,8 +365,12 @@
     for t, half in UNITS:
         for g in range(4):
             d2d(t, half, g).wait_send()
-            if g:
-                rs(t, half, g).wait_send()
+    for t, half in UNITS[:3]:
+        to_first(t, half, 0).wait_send()
+        to_first(t, half, 1).wait_send()
+        to_second(t, half).wait_send()
+    for g in (1, 2, 3):
+        rs(0, 0, g).wait_send()
 
 
 FIN = ((0, 1536), (1536, 2560), (2560, 3584))
@@ -366,8 +414,8 @@
                 V((ROWS, 3 * HALF), BF16),
                 V((TOK, HE), BF16), V((TOK, HE), BF16), V((2, ROWS, 1), F32),
                 V((2, 2, HALF, E), F32),
-                V((2, 2, 4, PIECE, E), F32), V((2, 2, 4, PIECE, E), F32), V((2, 2, 4, PIECE, E), F32),
-                dma((KSPLIT, 3)), dma((HEADS,)), dma((HEADS,)), dma,
+                V((2, 2, 4, PIECE, E), F32), V((2, 2, 4, PIECE, E), F32), V((2, 2, 4, PIECE, E), F32), V((2, 2, PIECE, E), F32),
+                dma((len(KPARTS), 3)), dma((HEADS,)), dma((HEADS,)), dma,
                 dma((NDEV,)), dma((NDEV,)), dma((2, NDEV)), dma((2, NDEV)),
                 dma((2, 2, 4)), dma((2, 2, 4)), dma((2, 2, 4)), dma((2, 2, 4)),
             ],

time: 30.5 us -> 29.5 us (0.967)
  Pallas kernels: 29.7 us -> 28.7 us
    pallas_call x1, Pallas kernels: 28.2 us -> 27.1 us  [local_layer(): pl.pallas_call(main_kernel, out_shape=(V((TOK, D), BF16), V((TOK, D), F32...]
where the time goes in v4:
time: 29.5 us; the launch traced here: 29.3 us
  Pallas kernels  28.7 us (97%)
  between operations  0.64 us (2%)
    pallas_call x1, Pallas kernels, local_layer(): pl.pallas_call(main_kernel, out_shape=(V((TOK, D), BF16), V((TOK, D), F32...  27.1 us
    pallas_call x1, Pallas kernels, local_layer(): pl.pallas_call(final_kernel, out_shape=(sds((TOK, D), BF16), sds((TOK, D)...  1.56 us

profile of v4, /device:TPU:0, one launch (start us, length us, event | category | flops | bytes accessed | tf_op | source)
XLA Modules:
  0.0 29.3 jit_solution(1477484079192615490)
XLA Ops:
  0.6 27.1 %shard_map.86 = (bf16[192,3584]{1,0:T(8,128)(2,1)S(1)}, f32[192,3584]{1,0:T(8,128)S(1)}, bf16[192,256]{1,0:T(8,128)(2,1)S(1)}, bf16[2,3584,128]{2,1,0:T(8,128)(2,1)S(1)}) custom-call(bf16[192,3584]{1,0:T(8,128)(2,1)} %x_hbm.1, bf16[192,3584]{1,0:T(8,128)(2,1)} %dy_hbm.1, s32[1,192]{1,0:T(1,128)} %bitcast.9, bf16[7,3584,128]{2,1,0:T(8,128)(2,1)} %bitcast.5, ...), custom_call_target="tpu_custom_call" | custom-call | tf_op jit(solution)/shard_map/pallas_call | solution.py:403
  27.8 1.6 %shard_map.87 = (bf16[192,3584]{1,0:T(8,128)(2,1)}, bf16[192,3584]{1,0:T(8,128)(2,1)}) custom-call(bf16[192,3584]{1,0:T(8,128)(2,1)S(1)} %get-tuple-element.6.y_s, f32[192,3584]{1,0:T(8,128)S(1)} %get-tuple-element.7.dx_s, bf16[192,256]{1,0:T(8,128)(2,1)S(1)} %get-tuple-element.8.dkv_s, bf16[2,3584,128]{2,1,0:T(8,128)(2,1)S(1)} %get-tuple-element.9.wkv_s), custom_call_target="tpu_custom_call" | custom-call | tf_op jit(solution)/shard_map/pallas_call | solution.py:426

commit v5 on v4

--- a/solution.py
+++ b/solution.py
@@ -44,7 +44,7 @@
                 s_s, p_s, dp_s, ds_s, o_s, dq_s, delta_s,
                 acc_s, rb1, comb, rb2, relay,
                 in_sem, wq_sem, wo_sem, dy_sem,
-                doc_send, doc_recv, kv_send, kv_recv,
+                doc_send, doc_recv, kv_send, kv_recv, kv_pass,
                 d2d_send, d2d_recv, rs_send, rs_recv):
     me = lax.axis_index('cp')
     core = lax.rem(me, 2)
@@ -72,10 +72,10 @@
     ld_wq = [pltpu.make_async_copy(wq_hbm.at[h], wq_s.at[h], wq_sem.at[h]) for h in range(HEADS)]
     ld_wo = [pltpu.make_async_copy(wo_hbm.at[h * E:(h + 1) * E], wo_s.at[h * E:(h + 1) * E], wo_sem.at[h])
              for h in range(HEADS)]
-    for part in ld_in + [ld_wq[:1]]:
+    for part in ld_in + [ld_wq[:2]]:
         for c in part:
             c.start()
-    LATER = (ld_wq[1:3], ld_wq[3:4], ld_wq[4:], [])
+    LATER = (ld_wq[2:4], ld_wq[4:], [ld_dy], ld_wo[:4])
 
     barrier = pltpu.get_barrier_semaphore()
     for r in range(1, NDEV):
@@ -86,7 +86,8 @@
             c.wait()
         for c in LATER[i]:
             c.start()
-        kv_part = dot(x_s[:, ka:kb], side_by_side(wkv_s, 0, 2, ka, kb))
+        kv_part = jnp.concatenate([dot(x_s[a:a + PIECE, ka:kb], side_by_side(wkv_s, 0, 2, ka, kb))
+                                   for a in (0, PIECE)], axis=0)
         if i:
             kv_part = s_s[0:TOK, 0:2 * E] + kv_part
         if i < len(KPARTS) - 1:
@@ -107,19 +108,42 @@
     def kv_blk(t, owner):
         return kv_s.at[t, :, pl.ds(pl.multiple_of(owner * PIECE, 32), PIECE), :]
 
-    kv_out = {}
+    def kv_send_own(t, g):
+        blk = kv_blk(t, me)
+        to = dev(2 * g) + 1 - core if g else dev(1)
+        return pltpu.make_async_remote_copy(
+            src_ref=blk, dst_ref=blk, send_sem=kv_send.at[t, g], recv_sem=kv_recv.at[t, 2 * g + core],
+            device_id={'cp': to}, device_id_type=pl.DeviceIdType.MESH)
+
+    def kv_hand_on(t, g, c):
+        blk = kv_blk(t, dev(2 * g) - core + c)
+        return pltpu.make_async_remote_copy(
+            src_ref=blk, dst_ref=blk, send_sem=kv_pass.at[t, 2 * g + c], recv_sem=kv_recv.at[t, 2 * g + c],
+            device_id={'cp': dev(1)}, device_id_type=pl.DeviceIdType.MESH)
+
+    REMOTE = [(g, c) for g in (3, 1, 2) for c in (1, 0)]
+
     for t in range(2):
-        for r in (6, 2, 4, 1):
-            kv_out[t, r] = rcopy(kv_blk(t, me), kv_blk(t, me), kv_send.at[t, r], kv_recv.at[t, r], r)
-            kv_out[t, r].start()
-
-    def kv_in(t, r):
-        return rcopy(kv_blk(t, dev(r)), kv_blk(t, dev(r)), kv_send.at[t, r], kv_recv.at[t, r], r)
-
-    def forward(t, r):
-        kv_in(t, r).wait_recv()
-        kv_out[t, r + 1] = rcopy(kv_blk(t, dev(r)), kv_blk(t, dev(r)), kv_send.at[t, r + 1], kv_recv.at[t, r + 1], 1)
-        kv_out[t, r + 1].start()
+        for g in (3, 1, 2, 0):
+            kv_send_own(t, g).start()
+
+    def hand_on(t):
+        @pl.when(core == 1)
+        def _():
+            for g, c in REMOTE:
+                kv_hand_on(t, g, c).wait_recv()
+                kv_hand_on(t, g, c).start()
+
+    def wait_blocks(t):
+        @pl.when(core == 0)
+        def _():
+            for g, c in REMOTE:
+                kv_hand_on(t, g, c).wait_recv()
+            kv_hand_on(t, 0, 1).wait_recv()
+
+        @pl.when(core == 1)
+        def _():
+            kv_hand_on(t, 0, 0).wait_recv()
 
     def put_rows(dst, val, h):
         dst[0, h * PIECE:(h + 1) * PIECE, :] = val[0:PIECE]
@@ -128,7 +152,7 @@
     for h0, h1 in GROUPS:
         for h in range(h0, h1):
             ld_wq[h].wait()
-        for c in ([ld_dy] + ld_wo[:4] if h0 == 0 else ld_wo[4:]):
+        for c in ld_wo[4:] if h0 == 0 else []:
             c.start()
         val = dot(x_s[...], side_by_side(wq_s, h0, h1, 0, D)).astype(BF16)
         for h in range(h0, h1):
@@ -163,43 +187,44 @@
             cap_s[:, 0:HALF] = cap_of(kpos_lo, first[PIECE:TOK], pos_hi)
             cap_s[:, HALF:2 * HALF] = cap_of(kpos_hi, first[PIECE:TOK], pos_hi)
             cap_s[:, 2 * HALF:3 * HALF] = cap_of(kpos_lo, first[0:PIECE], pos_lo)
-            for r in (6, 2, 4):
-                forward(0, r)
+            hand_on(0)
         else:
             for piece in range(2):
                 qt_s[piece] = q_s[piece].T
 
-    for r in (1, 7, 3, 5):
-        kv_in(0, r).wait_recv()
+    wait_blocks(0)
 
     k_scale = E ** -0.5
     exp_scale = k_scale * math.log2(math.e)
-    plan = ((1, SEQ, 0), (0, HALF, SEQ))
-
-    def spans(n, step=512):
-        return [(h + a, h + min(a + step, HALF)) for h in range(0, n, HALF) for a in range(0, HALF, step)]
-
     def keys(t, a, b):
         return kv_s[t, a // HALF, a % HALF:a % HALF + (b - a), :]
 
-    def over_keys(src, t, r0, r1, base, n):
+    def over_keys(src, t, base, segs):
         parts = []
-        for a, b in ((r0, (r0 + r1) // 2), ((r0 + r1) // 2, r1)):
-            acc = dot(src[a:b, base:base + HALF], kv_s[t, 0])
-            if n == SEQ:
-                acc = acc + dot(src[a:b, base + HALF:base + SEQ], kv_s[t, 1])
+        for a, b in ((0, ROWS // 2), (ROWS // 2, ROWS)):
+            acc = None
+            for c, d in segs:
+                val = dot(src[a:b, base + c:base + d], keys(t, c, d))
+                acc = val if acc is None else acc + val
             parts.append(acc)
         return jnp.concatenate(parts, axis=0)
 
-    def softmax(piece, n, base, h):
-        rb = 16 if n == SEQ else 32
+    def side(ref, rows, base, segs):
+        return jnp.concatenate([ref[rows, base + c:base + d] for c, d in segs], axis=1)
+
+    def softmax(base, segs, h):
+        rb = 16 if sum(d - c for c, d in segs) > HALF else 32
         for b in range(PIECE // rb):
-            r0 = h * PIECE + b * rb
-            s = jnp.minimum(s_s[r0:r0 + rb, base:base + n], cap_s[b * rb:(b + 1) * rb, base:base + n])
+            rows = slice(h * PIECE + b * rb, h * PIECE + (b + 1) * rb)
+            s = jnp.minimum(side(s_s, rows, base, segs), side(cap_s, slice(b * rb, (b + 1) * rb), base, segs))
             m = jnp.max(s, axis=1, keepdims=True)
             e = jnp.exp2((s - m) * exp_scale)
             l = jnp.sum(e, axis=1, keepdims=True)
-            p_s[r0:r0 + rb, base:base + n] = (e * (1.0 / l)).astype(BF16)
+            p = (e * (1.0 / l)).astype(BF16)
+            at = 0
+            for c, d in segs:
+                p_s[rows, base + c:base + d] = p[:, at:at + d - c]
+                at += d - c
 
     def blk(t, half, owner):
         return acc_s.at[t, half, pl.ds(pl.multiple_of(owner * PIECE, 32), PIECE), :]
@@ -211,20 +236,24 @@
     def rs(t, half, g):
         return rcopy(comb.at[t, half, g], rb2.at[t, half, g], rs_send.at[t, half, g], rs_recv.at[t, half, g], 2 * g)
 
-    def start_d2d(t, half):
-        for g in (3, 1, 2, 0):
+    def start_d2d(t, half, gs):
+        for g in gs:
             d2d(t, half, g).start()
 
-    def add_peer(t, half, g):
+    def add_peer(t, half, g, late):
+        if half and late and g >= 2:
+            comb[t, half, g] = jnp.zeros((PIECE, E), F32)
+            return
         d2d(t, half, g).wait_recv()
         comb[t, half, g] = (acc_s[t, half, pl.ds(pl.multiple_of(dev(2 * g) * PIECE, 32), PIECE), :]
                             + rb1[t, half, g])
 
-    def combine_direct(t, half):
+    def combine_direct(t, half, late):
         for g in (3, 1, 2, 0):
-            add_peer(t, half, g)
-            if g:
-                rs(t, half, g).start()
+            if not (half and late and g >= 2):
+                add_peer(t, half, g, late)
+                if g:
+                    rs(t, half, g).start()
 
     first_dev = lax.rem(cy + core, 2) * 4 + lax.rem(cx + 1 - core, 2) * 2 + core
     second_dev = lax.rem(cy + 1 - core, 2) * 4 + lax.rem(cx + core, 2) * 2 + core
@@ -244,95 +273,103 @@
             src_ref=comb.at[t, half, second_g], dst_ref=rb2.at[t, half, 2], send_sem=rs_send.at[t, half, 2],
             recv_sem=rs_recv.at[t, half, 2], device_id={'cp': second_dev}, device_id_type=pl.DeviceIdType.MESH)
 
-    def combine_relayed(t, half):
-        add_peer(t, half, 3)
+    def combine_relayed(t, half, late):
+        add_peer(t, half, 3, late)
         to_first(t, half, 0).start()
-        add_peer(t, half, 1)
-        add_peer(t, half, 2)
+        add_peer(t, half, 1, late)
+        add_peer(t, half, 2, late)
         to_first(t, half, 1).start()
-        add_peer(t, half, 0)
+        add_peer(t, half, 0, late)
 
     def pass_on(t, half):
         to_first(t, half, 0).wait_recv()
         comb[t, half, second_g] = comb[t, half, second_g] + relay[t, half]
         to_second(t, half).start()
 
-    def grad(t, half, lhs_t, src):
-        for a, b in spans(HALF, 256):
-            val = dot(lhs_t[1], src[:, half * HALF + a:half * HALF + b])
-            if half == 0:
-                val = val + dot(lhs_t[0], src[:, SEQ + a:SEQ + b])
-            acc_s[t, half, a:b, :] = val.T
-
-    def s_part(piece, base, a, b):
-        s_s[:, base + a:base + b] = dot(q_s[piece], keys(0, a, b), NT)
-
-    def dp_part(piece, base, a, b):
-        dp_s[:, base + a:base + b] = dot(do_s[piece], keys(1, a, b), NT)
-
-    def o_part(piece, base, n, r0, r1):
-        h0, h1 = r0 // PIECE, r1 // PIECE
-        o_bf = over_keys(p_s, 1, r0, r1, base, n).astype(BF16)
-        delta_s[piece, r0:r1, :] = jnp.sum(do_s[piece, r0:r1, :].astype(F32) * o_bf.astype(F32), axis=1, keepdims=True)
-        for h in range(h0, h1):
-            o_s[piece * PIECE:(piece + 1) * PIECE, h * E:(h + 1) * E] = o_bf[(h - h0) * PIECE:(h - h0 + 1) * PIECE]
-
-    def ds_rows(piece, base, a, b):
-        for h in range(HEADS):
-            for c in range(PIECE // 32):
-                r0 = h * PIECE + c * 32
-                ds_s[r0:r0 + 32, base + a:base + b] = (
-                    p_s[r0:r0 + 32, base + a:base + b].astype(F32)
-                    * (dp_s[r0:r0 + 32, base + a:base + b] - delta_s[piece, r0:r0 + 32, :])).astype(BF16)
-
-    def dq_part(piece, base, n):
-        dq_bf = (over_keys(ds_s, 0, 0, ROWS, base, n) * k_scale).astype(BF16)
-        for h in range(HEADS):
-            dq_s[piece * PIECE:(piece + 1) * PIECE, h * E:(h + 1) * E] = dq_bf[h * PIECE:(h + 1) * PIECE]
-
-    def softmax_with(piece, n, base, h0, h1, others):
-        for h in range(h0, h1):
-            softmax(piece, n, base, h)
-            left = h1 - h
-            take = -(-len(others) // left)
-            for fn in others[:take]:
-                fn()
-            others = others[take:]
-
-    for a, b in spans(SEQ):
-        s_part(1, 0, a, b)
-    for piece in range(2):
-        dot_s[piece] = do_s[piece].T
-    softmax_with(1, SEQ, 0, 0, 4, [lambda a=a, b=b: s_part(0, SEQ, a, b) for a, b in spans(HALF, 256)])
-    for r in (6, 2, 4):
-        forward(1, r)
-    softmax_with(1, SEQ, 0, 4, HEADS, [])
-    grad(1, 1, dot_s, p_s)
-    start_d2d(1, 1)
-    for r in (1, 7, 3, 5):
-        kv_in(1, r).wait_recv()
-    softmax_with(0, HALF, SEQ, 0, HEADS, [lambda a=a, b=b: dp_part(1, 0, a, b) for a, b in spans(SEQ, 256)])
-    combine_relayed(1, 1)
-    grad(1, 0, dot_s, p_s)
-    start_d2d(1, 0)
-    o_part(1, 0, SEQ, 0, ROWS)
-    ds_rows(1, 0, HALF, SEQ)
-    for a, b in spans(HALF):
-        dp_part(0, SEQ, a, b)
-    grad(0, 1, qt_s, ds_s)
-    start_d2d(0, 1)
-    combine_relayed(1, 0)
-    o_part(0, SEQ, HALF, 0, ROWS)
-    ds_rows(1, 0, 0, HALF)
-    ds_rows(0, SEQ, 0, HALF)
-    grad(0, 0, qt_s, ds_s)
-    start_d2d(0, 0)
-    pass_on(1, 1)
-    combine_relayed(0, 1)
-    for piece, n, base in plan:
-        dq_part(piece, base, n)
-
-    combine_direct(0, 0)
+    QUART = HALF // 2
+
+    def attention(late):
+        hi = ((0, HALF), (HALF + QUART, SEQ)) if late else ((0, HALF), (HALF, SEQ))
+        lo = ((0, HALF),) if late else ((0, QUART),)
+        hi_blocks = [(a, min(a + 512, d)) for c, d in hi for a in range(c, d, 512)]
+        lo_blocks = [(a, min(a + 512, d)) for c, d in lo for a in range(c, d, 512)]
+
+        def grad(t, half, lhs_t, src):
+            cuts = ((QUART, 512), (512, HALF)) if half and late else ((0, 256), (256, 512), (512, HALF))
+            for a, b in cuts:
+                val = dot(lhs_t[1], src[:, half * HALF + a:half * HALF + b])
+                c = b if late else min(b, QUART)
+                if not half and c > a:
+                    more = dot(lhs_t[0], src[:, SEQ + a:SEQ + c])
+                    val = val + more if c == b else jnp.concatenate([val[:, :c - a] + more, val[:, c - a:]], axis=1)
+                acc_s[t, half, a:b, :] = val.T
+            start_d2d(t, half, (1, 0) if half and late else (3, 1, 2, 0))
+
+        def s_part(piece, base, a, b, r0=0, r1=ROWS):
+            s_s[r0:r1, base + a:base + b] = dot(q_s[piece, r0:r1, :], keys(0, a, b), NT)
+
+        def dp_part(piece, base, a, b):
+            dp_s[:, base + a:base + b] = dot(do_s[piece], keys(1, a, b), NT)
+
+        def o_part(piece, base, segs):
+            o_bf = over_keys(p_s, 1, base, segs).astype(BF16)
+            delta_s[piece] = jnp.sum(do_s[piece].astype(F32) * o_bf.astype(F32), axis=1, keepdims=True)
+            for h in range(HEADS):
+                o_s[piece * PIECE:(piece + 1) * PIECE, h * E:(h + 1) * E] = o_bf[h * PIECE:(h + 1) * PIECE]
+
+        def ds_rows(piece, base, segs):
+            for h in range(HEADS):
+                for c in range(PIECE // 32):
+                    r0 = h * PIECE + c * 32
+                    for a, b in segs:
+                        ds_s[r0:r0 + 32, base + a:base + b] = (
+                            p_s[r0:r0 + 32, base + a:base + b].astype(F32)
+                            * (dp_s[r0:r0 + 32, base + a:base + b] - delta_s[piece, r0:r0 + 32, :])).astype(BF16)
+
+        def dq_part(piece, base, segs):
+            dq_bf = (over_keys(ds_s, 0, base, segs) * k_scale).astype(BF16)
+            for h in range(HEADS):
+                dq_s[piece * PIECE:(piece + 1) * PIECE, h * E:(h + 1) * E] = dq_bf[h * PIECE:(h + 1) * PIECE]
+
+        def softmax_with(base, segs, h0, h1, others):
+            for h in range(h0, h1):
+                softmax(base, segs, h)
+                left = h1 - h
+                take = -(-len(others) // left)
+                for fn in others[:take]:
+                    fn()
+                others = others[take:]
+
+        for a, b in hi_blocks:
+            s_part(1, 0, a, b, 0, 336)
+        for piece in range(2):
+            dot_s[piece] = do_s[piece].T
+        softmax_with(0, hi, 0, 3, [lambda a=a, b=b: s_part(1, 0, a, b, 336, ROWS) for a, b in hi_blocks])
+        hand_on(1)
+        softmax_with(0, hi, 3, HEADS, [lambda a=a, b=b: s_part(0, SEQ, a, b) for a, b in lo_blocks])
+        grad(1, 1, dot_s, p_s)
+        wait_blocks(1)
+        softmax_with(SEQ, lo, 0, HEADS, [lambda a=a, b=b: dp_part(1, 0, a, b) for a, b in hi_blocks])
+        combine_direct(1, 1, late)
+        grad(1, 0, dot_s, p_s)
+        o_part(1, 0, hi)
+        ds_rows(1, 0, hi[1:])
+        for a, b in lo_blocks:
+            dp_part(0, SEQ, a, b)
+        grad(0, 1, qt_s, ds_s)
+        combine_relayed(1, 0, late)
+        o_part(0, SEQ, lo)
+        ds_rows(1, 0, hi[:1])
+        ds_rows(0, SEQ, lo)
+        grad(0, 0, qt_s, ds_s)
+        combine_relayed(0, 1, late)
+        dq_part(1, 0, hi)
+        dq_part(0, SEQ, lo)
+
+    for late in range(2):
+        pl.when(cy == late)(lambda late=late: attention(late))
+
+    combine_direct(0, 0, 0)
     NY = 896
 
     def y_part(a, b):
@@ -350,7 +387,18 @@
             tot = tot * k_scale
         dkv_s[half * PIECE:(half + 1) * PIECE, t * E:(t + 1) * E] = tot.astype(BF16)
 
-    for t, half in UNITS[:3]:
+    @pl.when(cy == 0)
+    def _():
+        rs(1, 1, 1).wait_recv()
+        put_total(1, 1, comb[1, 1, 0] + rb2[1, 1, 1])
+
+    @pl.when(cy == 1)
+    def _():
+        for g in (1, 2, 3):
+            rs(1, 1, g).wait_recv()
+        put_total(1, 1, (comb[1, 1, 0] + rb2[1, 1, 1]) + (rb2[1, 1, 2] + rb2[1, 1, 3]))
+
+    for t, half in UNITS[1:3]:
         to_first(t, half, 1).wait_recv()
         to_second(t, half).wait_recv()
         put_total(t, half, comb[t, half, 0] + (rb2[t, half, 1] + rb2[t, half, 2]))
@@ -359,13 +407,34 @@
     put_total(0, 0, (comb[0, 0, 0] + rb2[0, 0, 1]) + (rb2[0, 0, 2] + rb2[0, 0, 3]))
 
     for r in range(1, NDEV):
-        kv_out[0, r].wait_send()
-        kv_out[1, r].wait_send()
         doc_out[r].wait_send()
+    for t in range(2):
+        for g in range(4):
+            kv_send_own(t, g).wait_send()
+
+    @pl.when(core == 1)
+    def _():
+        for t in range(2):
+            for g, c in REMOTE:
+                kv_hand_on(t, g, c).wait_send()
+
     for t, half in UNITS:
-        for g in range(4):
+        for g in range(2):
             d2d(t, half, g).wait_send()
-    for t, half in UNITS[:3]:
+        if not half:
+            for g in range(2, 4):
+                d2d(t, half, g).wait_send()
+    rs(1, 1, 1).wait_send()
+
+    @pl.when(cy == 0)
+    def _():
+        for t in range(2):
+            for g in range(2, 4):
+                d2d(t, 1, g).wait_send()
+        for g in range(2, 4):
+            rs(1, 1, g).wait_send()
+
+    for t, half in UNITS[1:3]:
         to_first(t, half, 0).wait_send()
         to_first(t, half, 1).wait_send()
         to_second(t, half).wait_send()
@@ -416,7 +485,7 @@
                 V((2, 2, HALF, E), F32),
                 V((2, 2, 4, PIECE, E), F32), V((2, 2, 4, PIECE, E), F32), V((2, 2, 4, PIECE, E), F32), V((2, 2, PIECE, E), F32),
                 dma((len(KPARTS), 3)), dma((HEADS,)), dma((HEADS,)), dma,
-                dma((NDEV,)), dma((NDEV,)), dma((2, NDEV)), dma((2, NDEV)),
+                dma((NDEV,)), dma((NDEV,)), dma((2, 4)), dma((2, NDEV)), dma((2, NDEV)),
                 dma((2, 2, 4)), dma((2, 2, 4)), dma((2, 2, 4)), dma((2, 2, 4)),
             ],
             compiler_params=pltpu.CompilerParams(collective_id=0, has_side_effects=True,

time: 29.5 us -> 28.2 us (0.956)
  Pallas kernels: 28.7 us -> 27.3 us
    pallas_call x1, Pallas kernels: 27.1 us -> 25.8 us  [local_layer(): pl.pallas_call(main_kernel, out_shape=(V((TOK, D), BF16), V((TOK, D), F32...]
where the time goes in v5:
time: 28.2 us; the launch traced here: 28.1 us
  Pallas kernels  27.3 us (97%)
  between operations  0.8 us (3%)
    pallas_call x1, Pallas kernels, local_layer(): pl.pallas_call(main_kernel, out_shape=(V((TOK, D), BF16), V((TOK, D), F32...  25.8 us
    pallas_call x1, Pallas kernels, local_layer(): pl.pallas_call(final_kernel, out_shape=(sds((TOK, D), BF16), sds((TOK, D)...  1.56 us

profile of v5, /device:TPU:0, one launch (start us, length us, event | category | flops | bytes accessed | tf_op | source)
XLA Modules:
  0.0 28.1 jit_solution(3281240259696035640)
XLA Ops:
  0.6 25.8 %shard_map.86 = (bf16[192,3584]{1,0:T(8,128)(2,1)S(1)}, f32[192,3584]{1,0:T(8,128)S(1)}, bf16[192,256]{1,0:T(8,128)(2,1)S(1)}, bf16[2,3584,128]{2,1,0:T(8,128)(2,1)S(1)}) custom-call(bf16[192,3584]{1,0:T(8,128)(2,1)} %x_hbm.1, bf16[192,3584]{1,0:T(8,128)(2,1)} %dy_hbm.1, s32[1,192]{1,0:T(1,128)} %bitcast.9, bf16[7,3584,128]{2,1,0:T(8,128)(2,1)} %bitcast.5, ...), custom_call_target="tpu_custom_call" | custom-call | tf_op jit(solution)/shard_map/pallas_call | solution.py:472
  26.4 1.6 %shard_map.87 = (bf16[192,3584]{1,0:T(8,128)(2,1)}, bf16[192,3584]{1,0:T(8,128)(2,1)}) custom-call(bf16[192,3584]{1,0:T(8,128)(2,1)S(1)} %get-tuple-element.6.y_s, f32[192,3584]{1,0:T(8,128)S(1)} %get-tuple-element.7.dx_s, bf16[192,256]{1,0:T(8,128)(2,1)S(1)} %get-tuple-element.8.dkv_s, bf16[2,3584,128]{2,1,0:T(8,128)(2,1)S(1)} %get-tuple-element.9.wkv_s), custom_call_target="tpu_custom_call" | custom-call | tf_op jit(solution)/shard_map/pallas_call | solution.py:495

commit v6 on v5

--- a/solution.py
+++ b/solution.py
@@ -37,13 +37,13 @@
     return jnp.concatenate([ref[h, r0:r1, :] for h in range(h0, h1)], axis=1)
 
 
-def main_kernel(x_hbm, dy_hbm, doc_ref, wq_hbm, wk_hbm, wv_hbm, wo_hbm,
+def main_kernel(x_hbm, dy_hbm, doc_hbm, wq_hbm, wk_hbm, wv_hbm, wo_hbm,
                 y_s, dx_s, dkv_s, wkv_s,
-                x_s, dy_s, wq_s, wo_s,
+                x_s, dy_s, wq_s, wo_s, doc_ref,
                 kv_s, doc_s, q_s, do_s, qt_s, dot_s, cap_s,
                 s_s, p_s, dp_s, ds_s, o_s, dq_s, delta_s,
                 acc_s, rb1, comb, rb2, relay,
-                in_sem, wq_sem, wo_sem, dy_sem,
+                in_sem, wq_sem, wo_sem, dy_sem, doc_sem,
                 doc_send, doc_recv, kv_send, kv_recv, kv_pass,
                 d2d_send, d2d_recv, rs_send, rs_recv):
     me = lax.axis_index('cp')
@@ -69,10 +69,11 @@
                       pltpu.make_async_copy(wk_hbm.at[ks], wkv_s.at[0, ks], in_sem.at[i, 1]),
                       pltpu.make_async_copy(wv_hbm.at[ks], wkv_s.at[1, ks], in_sem.at[i, 2])])
     ld_dy = pltpu.make_async_copy(dy_hbm, dy_s, dy_sem)
+    ld_doc = pltpu.make_async_copy(doc_hbm, doc_ref, doc_sem)
     ld_wq = [pltpu.make_async_copy(wq_hbm.at[h], wq_s.at[h], wq_sem.at[h]) for h in range(HEADS)]
     ld_wo = [pltpu.make_async_copy(wo_hbm.at[h * E:(h + 1) * E], wo_s.at[h * E:(h + 1) * E], wo_sem.at[h])
              for h in range(HEADS)]
-    for part in ld_in + [ld_wq[:2]]:
+    for part in ld_in + [[ld_doc], ld_wq[:2]]:
         for c in part:
             c.start()
     LATER = (ld_wq[2:4], ld_wq[4:], [ld_dy], ld_wo[:4])
@@ -94,6 +95,7 @@
             s_s[0:TOK, 0:2 * E] = kv_part
         if i == 1:
             pl.semaphore_wait(barrier, NDEV - 1)
+            ld_doc.wait()
             doc_s[me] = doc_ref[...]
             doc_out = {}
             for r in range(1, NDEV):
@@ -297,8 +299,12 @@
         def grad(t, half, lhs_t, src):
             cuts = ((QUART, 512), (512, HALF)) if half and late else ((0, 256), (256, 512), (512, HALF))
             for a, b in cuts:
+                c = b if late else min(b, QUART)
+                if t == 0:
+                    ds_rows(1, 0, ((half * HALF + a, half * HALF + b),))
+                    if not half and c > a:
+                        ds_rows(0, SEQ, ((a, c),))
                 val = dot(lhs_t[1], src[:, half * HALF + a:half * HALF + b])
-                c = b if late else min(b, QUART)
                 if not half and c > a:
                     more = dot(lhs_t[0], src[:, SEQ + a:SEQ + c])
                     val = val + more if c == b else jnp.concatenate([val[:, :c - a] + more, val[:, c - a:]], axis=1)
@@ -350,17 +356,14 @@
         grad(1, 1, dot_s, p_s)
         wait_blocks(1)
         softmax_with(SEQ, lo, 0, HEADS, [lambda a=a, b=b: dp_part(1, 0, a, b) for a, b in hi_blocks])
+        grad(1, 0, dot_s, p_s)
         combine_direct(1, 1, late)
-        grad(1, 0, dot_s, p_s)
         o_part(1, 0, hi)
-        ds_rows(1, 0, hi[1:])
         for a, b in lo_blocks:
             dp_part(0, SEQ, a, b)
         grad(0, 1, qt_s, ds_s)
         combine_relayed(1, 0, late)
         o_part(0, SEQ, lo)
-        ds_rows(1, 0, hi[:1])
-        ds_rows(0, SEQ, lo)
         grad(0, 0, qt_s, ds_s)
         combine_relayed(0, 1, late)
         dq_part(1, 0, hi)
@@ -472,10 +475,10 @@
         parts = pl.pallas_call(
             main_kernel,
             out_shape=(V((TOK, D), BF16), V((TOK, D), F32), V((TOK, 2 * E), BF16), V((2, D, E), BF16)),
-            in_specs=[hbm_spec, hbm_spec, vmem_spec, hbm_spec, hbm_spec, hbm_spec, hbm_spec],
+            in_specs=[hbm_spec, hbm_spec, hbm_spec, hbm_spec, hbm_spec, hbm_spec, hbm_spec],
             out_specs=(vmem_spec,) * 4,
             scratch_shapes=[
-                V((TOK, D), BF16), V((TOK, D), BF16), V((HEADS, D, E), BF16), V((HE, D), BF16),
+                V((TOK, D), BF16), V((TOK, D), BF16), V((HEADS, D, E), BF16), V((HE, D), BF16), V((1, TOK), jnp.int32),
                 V((2, 2, HALF, E), BF16), V((NDEV, 1, TOK), jnp.int32),
                 V((2, ROWS, E), BF16), V((2, ROWS, E), BF16), V((2, E, ROWS), BF16), V((2, E, ROWS), BF16),
                 V((PIECE, 3 * HALF), F32),
@@ -484,13 +487,13 @@
                 V((TOK, HE), BF16), V((TOK, HE), BF16), V((2, ROWS, 1), F32),
                 V((2, 2, HALF, E), F32),
                 V((2, 2, 4, PIECE, E), F32), V((2, 2, 4, PIECE, E), F32), V((2, 2, 4, PIECE, E), F32), V((2, 2, PIECE, E), F32),
-                dma((len(KPARTS), 3)), dma((HEADS,)), dma((HEADS,)), dma,
+                dma((len(KPARTS), 3)), dma((HEADS,)), dma((HEADS,)), dma, dma,
                 dma((NDEV,)), dma((NDEV,)), dma((2, 4)), dma((2, NDEV)), dma((2, NDEV)),
                 dma((2, 2, 4)), dma((2, 2, 4)), dma((2, 2, 4)), dma((2, 2, 4)),
             ],
             compiler_params=pltpu.CompilerParams(collective_id=0, has_side_effects=True,
                                                  vmem_limit_bytes=50 * 1024 * 1024),
-        )(hbm(x_in), hbm(dy_in), doc_id.reshape(1, TOK), hbm(jnp.transpose(w_q, (1, 0, 2))), hbm(w_k.reshape(D, E)),
+        )(hbm(x_in), hbm(dy_in), hbm(doc_id.reshape(1, TOK)), hbm(jnp.transpose(w_q, (1, 0, 2))), hbm(w_k.reshape(D, E)),
           hbm(w_v.reshape(D, E)), hbm(w_o.reshape(HE, D)))
         return pl.pallas_call(
             final_kernel,

time: 28.2 us -> 27.3 us (0.968)
  Pallas kernels: 27.3 us -> 26.4 us
    pallas_call x1, Pallas kernels: 25.8 us -> 24.8 us  [local_layer(): pl.pallas_call(main_kernel, out_shape=(V((TOK, D), BF16), V((TOK, D), F32...]
where the time goes in v6:
time: 27.3 us; the launch traced here: 27.2 us
  Pallas kernels  26.4 us (97%)
  between operations  0.8 us (3%)
    pallas_call x1, Pallas kernels, local_layer(): pl.pallas_call(main_kernel, out_shape=(V((TOK, D), BF16), V((TOK, D), F32...  24.8 us
    pallas_call x1, Pallas kernels, local_layer(): pl.pallas_call(final_kernel, out_shape=(sds((TOK, D), BF16), sds((TOK, D)...  1.56 us

profile of v6, /device:TPU:0, one launch (start us, length us, event | category | flops | bytes accessed | tf_op | source)
XLA Modules:
  0.0 27.2 jit_solution(18177429235834420123)
XLA Ops:
  0.6 24.8 %shard_map.86 = (bf16[192,3584]{1,0:T(8,128)(2,1)S(1)}, f32[192,3584]{1,0:T(8,128)S(1)}, bf16[192,256]{1,0:T(8,128)(2,1)S(1)}, bf16[2,3584,128]{2,1,0:T(8,128)(2,1)S(1)}) custom-call(bf16[192,3584]{1,0:T(8,128)(2,1)} %x_hbm.1, bf16[192,3584]{1,0:T(8,128)(2,1)} %dy_hbm.1, s32[1,192]{1,0:T(1,128)} %bitcast.9, bf16[7,3584,128]{2,1,0:T(8,128)(2,1)} %bitcast.5, ...), custom_call_target="tpu_custom_call" | custom-call | tf_op jit(solution)/shard_map/pallas_call | solution.py:475
  25.4 1.6 %shard_map.87 = (bf16[192,3584]{1,0:T(8,128)(2,1)}, bf16[192,3584]{1,0:T(8,128)(2,1)}) custom-call(bf16[192,3584]{1,0:T(8,128)(2,1)S(1)} %get-tuple-element.6.y_s, f32[192,3584]{1,0:T(8,128)S(1)} %get-tuple-element.7.dx_s, bf16[192,256]{1,0:T(8,128)(2,1)S(1)} %get-tuple-element.8.dkv_s, bf16[2,3584,128]{2,1,0:T(8,128)(2,1)S(1)} %get-tuple-element.9.wkv_s), custom_call_target="tpu_custom_call" | custom-call | tf_op jit(solution)/shard_map/pallas_call | solution.py:498

commit v7 on v6

--- a/solution.py
+++ b/solution.py
@@ -21,7 +21,7 @@
 ROWS = HEADS * PIECE
 HALF = NDEV * PIECE
 SEQ = 2 * HALF
-KPARTS = ((0, 1024), (1024, 2048), (2048, 3072), (3072, D))
+KPARTS = ((0, 2048), (2048, D))
 
 NT = (((1,), (1,)), ((), ()))
 NN = (((1,), (0,)), ((), ()))
@@ -70,13 +70,14 @@
                       pltpu.make_async_copy(wv_hbm.at[ks], wkv_s.at[1, ks], in_sem.at[i, 2])])
     ld_dy = pltpu.make_async_copy(dy_hbm, dy_s, dy_sem)
     ld_doc = pltpu.make_async_copy(doc_hbm, doc_ref, doc_sem)
-    ld_wq = [pltpu.make_async_copy(wq_hbm.at[h], wq_s.at[h], wq_sem.at[h]) for h in range(HEADS)]
-    ld_wo = [pltpu.make_async_copy(wo_hbm.at[h * E:(h + 1) * E], wo_s.at[h * E:(h + 1) * E], wo_sem.at[h])
-             for h in range(HEADS)]
-    for part in ld_in + [[ld_doc], ld_wq[:2]]:
+    ld_wq = [pltpu.make_async_copy(wq_hbm.at[a:b], wq_s.at[a:b], wq_sem.at[i])
+             for i, (a, b) in enumerate(((0, 2), (2, 4), (4, HEADS)))]
+    ld_wo = [pltpu.make_async_copy(wo_hbm.at[a * E:b * E], wo_s.at[a * E:b * E], wo_sem.at[i])
+             for i, (a, b) in enumerate(GROUPS)]
+    for part in ld_in + [[ld_doc], ld_wq[:1]]:
         for c in part:
             c.start()
-    LATER = (ld_wq[2:4], ld_wq[4:], [ld_dy], ld_wo[:4])
+    LATER = (ld_wq[1:2], ld_wq[2:] + [ld_dy])
 
     barrier = pltpu.get_barrier_semaphore()
     for r in range(1, NDEV):
@@ -93,13 +94,13 @@
             kv_part = s_s[0:TOK, 0:2 * E] + kv_part
         if i < len(KPARTS) - 1:
             s_s[0:TOK, 0:2 * E] = kv_part
-        if i == 1:
+        if i == 0:
             pl.semaphore_wait(barrier, NDEV - 1)
             ld_doc.wait()
             doc_s[me] = doc_ref[...]
             doc_out = {}
             for r in range(1, NDEV):
-                doc_out[r] = rcopy(doc_ref, doc_s.at[me], doc_send.at[r], doc_recv.at[r], r)
+                doc_out[r] = rcopy(doc_ref, doc_s.at[me], doc_send, doc_recv, r)
                 doc_out[r].start()
     kv_own = kv_part.astype(BF16)
     my_off = pl.multiple_of(me * PIECE, 32)
@@ -114,13 +115,13 @@
         blk = kv_blk(t, me)
         to = dev(2 * g) + 1 - core if g else dev(1)
         return pltpu.make_async_remote_copy(
-            src_ref=blk, dst_ref=blk, send_sem=kv_send.at[t, g], recv_sem=kv_recv.at[t, 2 * g + core],
+            src_ref=blk, dst_ref=blk, send_sem=kv_send.at[t, g], recv_sem=kv_recv.at[t, 2 * g - 1 + core if g else 0],
             device_id={'cp': to}, device_id_type=pl.DeviceIdType.MESH)
 
     def kv_hand_on(t, g, c):
         blk = kv_blk(t, dev(2 * g) - core + c)
         return pltpu.make_async_remote_copy(
-            src_ref=blk, dst_ref=blk, send_sem=kv_pass.at[t, 2 * g + c], recv_sem=kv_recv.at[t, 2 * g + c],
+            src_ref=blk, dst_ref=blk, send_sem=kv_pass.at[t], recv_sem=kv_recv.at[t, 2 * g - 1 + c if g else 0],
             device_id={'cp': dev(1)}, device_id_type=pl.DeviceIdType.MESH)
 
     REMOTE = [(g, c) for g in (3, 1, 2) for c in (1, 0)]
@@ -152,19 +153,17 @@
         dst[1, h * PIECE:(h + 1) * PIECE, :] = val[PIECE:TOK]
 
     for h0, h1 in GROUPS:
-        for h in range(h0, h1):
-            ld_wq[h].wait()
-        for c in ld_wo[4:] if h0 == 0 else []:
-            c.start()
+        for c in ld_wq[:2] if h0 == 0 else ld_wq[2:]:
+            c.wait()
+        ld_wo[0 if h0 == 0 else 1].start()
         val = dot(x_s[...], side_by_side(wq_s, h0, h1, 0, D)).astype(BF16)
         for h in range(h0, h1):
             put_rows(q_s, val[:, (h - h0) * E:(h - h0 + 1) * E], h)
-    for r in range(1, NDEV):
-        rcopy(doc_ref, doc_s.at[dev(r)], doc_send.at[r], doc_recv.at[r], r).wait_recv()
+    doc_sum = rcopy(doc_s.at[1:NDEV], doc_s.at[1:NDEV], doc_send, doc_recv, 1)
+    doc_sum.wait_recv()
     ld_dy.wait()
     for h0, h1 in GROUPS:
-        for h in range(h0, h1):
-            ld_wo[h].wait()
+        ld_wo[0 if h0 == 0 else 1].wait()
         val = dot(dy_s[...], wo_s[h0 * E:h1 * E, :], NT).astype(BF16)
         for h in range(h0, h1):
             put_rows(do_s, val[:, (h - h0) * E:(h - h0 + 1) * E], h)
@@ -228,29 +227,22 @@
                 p_s[rows, base + c:base + d] = p[:, at:at + d - c]
                 at += d - c
 
-    def blk(t, half, owner):
-        return acc_s.at[t, half, pl.ds(pl.multiple_of(owner * PIECE, 32), PIECE), :]
-
-    def d2d(t, half, g):
-        return rcopy(blk(t, half, dev(2 * g + 1)), rb1.at[t, half, g], d2d_send.at[t, half, g],
-                     d2d_recv.at[t, half, g], 1)
+    def d2d(t, half, late):
+        q = slice(2 if half and late else 0, 4)
+        return rcopy(acc_s.at[t, half, q, 1 - core], rb1.at[t, half, q], d2d_send.at[t, half], d2d_recv.at[t, half], 1)
 
     def rs(t, half, g):
-        return rcopy(comb.at[t, half, g], rb2.at[t, half, g], rs_send.at[t, half, g], rs_recv.at[t, half, g], 2 * g)
-
-    def start_d2d(t, half, gs):
-        for g in gs:
-            d2d(t, half, g).start()
+        return rcopy(comb.at[t, half, g], rb2.at[t, half, g], rs_send.at[t, half, g - 1], rs_recv.at[t, half, g - 1], 2 * g)
 
     def add_peer(t, half, g, late):
         if half and late and g >= 2:
             comb[t, half, g] = jnp.zeros((PIECE, E), F32)
             return
-        d2d(t, half, g).wait_recv()
-        comb[t, half, g] = (acc_s[t, half, pl.ds(pl.multiple_of(dev(2 * g) * PIECE, 32), PIECE), :]
-                            + rb1[t, half, g])
+        q = dev(2 * g) // 2
+        comb[t, half, g] = acc_s[t, half, q, core] + rb1[t, half, q]
 
     def combine_direct(t, half, late):
+        d2d(t, half, late).wait_recv()
         for g in (3, 1, 2, 0):
             if not (half and late and g >= 2):
                 add_peer(t, half, g, late)
@@ -276,6 +268,7 @@
             recv_sem=rs_recv.at[t, half, 2], device_id={'cp': second_dev}, device_id_type=pl.DeviceIdType.MESH)
 
     def combine_relayed(t, half, late):
+        d2d(t, half, late).wait_recv()
         add_peer(t, half, 3, late)
         to_first(t, half, 0).start()
         add_peer(t, half, 1, late)
@@ -308,8 +301,12 @@
                 if not half and c > a:
                     more = dot(lhs_t[0], src[:, SEQ + a:SEQ + c])
                     val = val + more if c == b else jnp.concatenate([val[:, :c - a] + more, val[:, c - a:]], axis=1)
-                acc_s[t, half, a:b, :] = val.T
-            start_d2d(t, half, (1, 0) if half and late else (3, 1, 2, 0))
+                val = val.T
+                for r in range(a - a % PIECE, b, PIECE):
+                    c, d = max(a, r), min(b, r + PIECE)
+                    slot = r // PIECE
+                    acc_s[t, half, slot // 2, slot % 2, c - r:d - r, :] = val[c - a:d - a]
+            d2d(t, half, late).start()
 
         def s_part(piece, base, a, b, r0=0, r1=ROWS):
             s_s[r0:r1, base + a:base + b] = dot(q_s[piece, r0:r1, :], keys(0, a, b), NT)
@@ -347,12 +344,12 @@
                 others = others[take:]
 
         for a, b in hi_blocks:
-            s_part(1, 0, a, b, 0, 336)
+            s_part(1, 0, a, b, 0, 192)
         for piece in range(2):
             dot_s[piece] = do_s[piece].T
-        softmax_with(0, hi, 0, 3, [lambda a=a, b=b: s_part(1, 0, a, b, 336, ROWS) for a, b in hi_blocks])
+        softmax_with(0, hi, 0, 2, [lambda a=a, b=b: s_part(1, 0, a, b, 192, ROWS) for a, b in hi_blocks])
         hand_on(1)
-        softmax_with(0, hi, 3, HEADS, [lambda a=a, b=b: s_part(0, SEQ, a, b) for a, b in lo_blocks])
+        softmax_with(0, hi, 2, HEADS, [lambda a=a, b=b: s_part(0, SEQ, a, b) for a, b in lo_blocks])
         grad(1, 1, dot_s, p_s)
         wait_blocks(1)
         softmax_with(SEQ, lo, 0, HEADS, [lambda a=a, b=b: dp_part(1, 0, a, b) for a, b in hi_blocks])
@@ -409,8 +406,7 @@
         rs(0, 0, g).wait_recv()
     put_total(0, 0, (comb[0, 0, 0] + rb2[0, 0, 1]) + (rb2[0, 0, 2] + rb2[0, 0, 3]))
 
-    for r in range(1, NDEV):
-        doc_out[r].wait_send()
+    doc_sum.wait_send()
     for t in range(2):
         for g in range(4):
             kv_send_own(t, g).wait_send()
@@ -418,24 +414,24 @@
     @pl.when(core == 1)
     def _():
         for t in range(2):
-            for g, c in REMOTE:
-                kv_hand_on(t, g, c).wait_send()
-
-    for t, half in UNITS:
-        for g in range(2):
-            d2d(t, half, g).wait_send()
-        if not half:
-            for g in range(2, 4):
-                d2d(t, half, g).wait_send()
+            six = kv_s.at[t, :, 0:6 * PIECE, :]
+            rcopy(six, six, kv_pass.at[t], kv_recv.at[t, 0], 1).wait_send()
+
+    for t in range(2):
+        d2d(t, 0, 0).wait_send()
     rs(1, 1, 1).wait_send()
 
     @pl.when(cy == 0)
     def _():
         for t in range(2):
-            for g in range(2, 4):
-                d2d(t, 1, g).wait_send()
+            d2d(t, 1, 0).wait_send()
         for g in range(2, 4):
             rs(1, 1, g).wait_send()
+
+    @pl.when(cy == 1)
+    def _():
+        for t in range(2):
+            d2d(t, 1, 1).wait_send()
 
     for t, half in UNITS[1:3]:
         to_first(t, half, 0).wait_send()
@@ -485,11 +481,11 @@
                 V((ROWS, 3 * HALF), F32), V((ROWS, 3 * HALF), BF16), V((ROWS, 3 * HALF), F32),
                 V((ROWS, 3 * HALF), BF16),
                 V((TOK, HE), BF16), V((TOK, HE), BF16), V((2, ROWS, 1), F32),
-                V((2, 2, HALF, E), F32),
+                V((2, 2, 4, 2, PIECE, E), F32),
                 V((2, 2, 4, PIECE, E), F32), V((2, 2, 4, PIECE, E), F32), V((2, 2, 4, PIECE, E), F32), V((2, 2, PIECE, E), F32),
-                dma((len(KPARTS), 3)), dma((HEADS,)), dma((HEADS,)), dma, dma,
-                dma((NDEV,)), dma((NDEV,)), dma((2, 4)), dma((2, NDEV)), dma((2, NDEV)),
-                dma((2, 2, 4)), dma((2, 2, 4)), dma((2, 2, 4)), dma((2, 2, 4)),
+                dma((len(KPARTS), 3)), dma((3,)), dma((2,)), dma, dma,
+                dma, dma, dma((2, 4)), dma((2, 7)), dma((2,)),
+                dma((2, 2)), dma((2, 2)), dma((2, 2, 3)), dma((2, 2, 3)),
             ],
             compiler_params=pltpu.CompilerParams(collective_id=0, has_side_effects=True,
                                                  vmem_limit_bytes=50 * 1024 * 1024),

time: 27.3 us -> 26.4 us (0.967)
  Pallas kernels: 26.4 us -> 25.5 us
    pallas_call x1, Pallas kernels: 24.8 us -> 23.9 us  [local_layer(): pl.pallas_call(main_kernel, out_shape=(V((TOK, D), BF16), V((TOK, D), F32...]
where the time goes in v7:
time: 26.4 us; the launch traced here: 26.3 us
  Pallas kernels  25.5 us (97%)
  between operations  0.8 us (3%)
    pallas_call x1, Pallas kernels, local_layer(): pl.pallas_call(main_kernel, out_shape=(V((TOK, D), BF16), V((TOK, D), F32...  23.9 us
    pallas_call x1, Pallas kernels, local_layer(): pl.pallas_call(final_kernel, out_shape=(sds((TOK, D), BF16), sds((TOK, D)...  1.56 us

profile of v7, /device:TPU:0, one launch (start us, length us, event | category | flops | bytes accessed | tf_op | source)
XLA Modules:
  0.0 26.3 jit_solution(4187202505553879809)
XLA Ops:
  0.6 23.9 %shard_map.86 = (bf16[192,3584]{1,0:T(8,128)(2,1)S(1)}, f32[192,3584]{1,0:T(8,128)S(1)}, bf16[192,256]{1,0:T(8,128)(2,1)S(1)}, bf16[2,3584,128]{2,1,0:T(8,128)(2,1)S(1)}) custom-call(bf16[192,3584]{1,0:T(8,128)(2,1)} %x_hbm.1, bf16[192,3584]{1,0:T(8,128)(2,1)} %dy_hbm.1, s32[1,192]{1,0:T(1,128)} %bitcast.9, bf16[7,3584,128]{2,1,0:T(8,128)(2,1)} %bitcast.5, ...), custom_call_target="tpu_custom_call" | custom-call | tf_op jit(solution)/shard_map/pallas_call | solution.py:471
  24.6 1.6 %shard_map.87 = (bf16[192,3584]{1,0:T(8,128)(2,1)}, bf16[192,3584]{1,0:T(8,128)(2,1)}) custom-call(bf16[192,3584]{1,0:T(8,128)(2,1)S(1)} %get-tuple-element.6.y_s, f32[192,3584]{1,0:T(8,128)S(1)} %get-tuple-element.7.dx_s, bf16[192,256]{1,0:T(8,128)(2,1)S(1)} %get-tuple-element.8.dkv_s, bf16[2,3584,128]{2,1,0:T(8,128)(2,1)S(1)} %get-tuple-element.9.wkv_s), custom_call_target="tpu_custom_call" | custom-call | tf_op jit(solution)/shard_map/pallas_call | solution.py:494

commit v8 on v7

--- a/solution.py
+++ b/solution.py
@@ -45,7 +45,7 @@
                 acc_s, rb1, comb, rb2, relay,
                 in_sem, wq_sem, wo_sem, dy_sem, doc_sem,
                 doc_send, doc_recv, kv_send, kv_recv, kv_pass,
-                d2d_send, d2d_recv, rs_send, rs_recv):
+                d2d_send, d2d_recv, rs_send, rs_recv, relay_recv):
     me = lax.axis_index('cp')
     core = lax.rem(me, 2)
     chip = me // 2
@@ -115,16 +115,12 @@
         blk = kv_blk(t, me)
         to = dev(2 * g) + 1 - core if g else dev(1)
         return pltpu.make_async_remote_copy(
-            src_ref=blk, dst_ref=blk, send_sem=kv_send.at[t, g], recv_sem=kv_recv.at[t, 2 * g - 1 + core if g else 0],
+            src_ref=blk, dst_ref=blk, send_sem=kv_send.at[t], recv_sem=kv_recv.at[t, 1 if g else 0],
             device_id={'cp': to}, device_id_type=pl.DeviceIdType.MESH)
 
-    def kv_hand_on(t, g, c):
-        blk = kv_blk(t, dev(2 * g) - core + c)
-        return pltpu.make_async_remote_copy(
-            src_ref=blk, dst_ref=blk, send_sem=kv_pass.at[t], recv_sem=kv_recv.at[t, 2 * g - 1 + c if g else 0],
-            device_id={'cp': dev(1)}, device_id_type=pl.DeviceIdType.MESH)
-
-    REMOTE = [(g, c) for g in (3, 1, 2) for c in (1, 0)]
+    def kv_sum(t, n):
+        blks = kv_s.at[t, :, 0:n * PIECE, :]
+        return rcopy(blks, blks, kv_pass.at[t], kv_recv.at[t, 1], 1)
 
     for t in range(2):
         for g in (3, 1, 2, 0):
@@ -133,20 +129,16 @@
     def hand_on(t):
         @pl.when(core == 1)
         def _():
-            for g, c in REMOTE:
-                kv_hand_on(t, g, c).wait_recv()
-                kv_hand_on(t, g, c).start()
+            kv_sum(t, 6).wait_recv()
+            for g in (3, 1, 2):
+                both = kv_s.at[t, :, pl.ds(pl.multiple_of((dev(2 * g) - core) * PIECE, 64), 2 * PIECE), :]
+                rcopy(both, both, kv_pass.at[t], kv_recv.at[t, 1], 1).start()
 
     def wait_blocks(t):
         @pl.when(core == 0)
         def _():
-            for g, c in REMOTE:
-                kv_hand_on(t, g, c).wait_recv()
-            kv_hand_on(t, 0, 1).wait_recv()
-
-        @pl.when(core == 1)
-        def _():
-            kv_hand_on(t, 0, 0).wait_recv()
+            kv_sum(t, 6).wait_recv()
+        rcopy(kv_blk(t, dev(1)), kv_blk(t, dev(1)), kv_send.at[t], kv_recv.at[t, 0], 1).wait_recv()
 
     def put_rows(dst, val, h):
         dst[0, h * PIECE:(h + 1) * PIECE, :] = val[0:PIECE]
@@ -232,7 +224,7 @@
         return rcopy(acc_s.at[t, half, q, 1 - core], rb1.at[t, half, q], d2d_send.at[t, half], d2d_recv.at[t, half], 1)
 
     def rs(t, half, g):
-        return rcopy(comb.at[t, half, g], rb2.at[t, half, g], rs_send.at[t, half, g - 1], rs_recv.at[t, half, g - 1], 2 * g)
+        return rcopy(comb.at[t, half, g], rb2.at[t, half, g], rs_send.at[1 - t * half], rs_recv.at[t, half], 2 * g)
 
     def add_peer(t, half, g, late):
         if half and late and g >= 2:
@@ -240,6 +232,10 @@
             return
         q = dev(2 * g) // 2
         comb[t, half, g] = acc_s[t, half, q, core] + rb1[t, half, q]
+
+    def rs_sum(t, half, n):
+        blks = rb1.at[0, 0, 0:n]
+        return rcopy(blks, blks, rs_send.at[1 - t * half], rs_recv.at[t, half], 2)
 
     def combine_direct(t, half, late):
         d2d(t, half, late).wait_recv()
@@ -255,17 +251,17 @@
 
     def to_first(t, half, i):
         if i == 0:
-            src, dst = comb.at[t, half, 3], relay.at[t, half]
+            src, dst, sem = comb.at[t, half, 3], relay.at[t, half], relay_recv.at[t]
         else:
-            src, dst = comb.at[t, half, first_g], rb2.at[t, half, 1]
+            src, dst, sem = comb.at[t, half, first_g], rb2.at[t, half, 1], rs_recv.at[t, half]
         return pltpu.make_async_remote_copy(
-            src_ref=src, dst_ref=dst, send_sem=rs_send.at[t, half, i], recv_sem=rs_recv.at[t, half, i],
+            src_ref=src, dst_ref=dst, send_sem=rs_send.at[1], recv_sem=sem,
             device_id={'cp': first_dev}, device_id_type=pl.DeviceIdType.MESH)
 
     def to_second(t, half):
         return pltpu.make_async_remote_copy(
-            src_ref=comb.at[t, half, second_g], dst_ref=rb2.at[t, half, 2], send_sem=rs_send.at[t, half, 2],
-            recv_sem=rs_recv.at[t, half, 2], device_id={'cp': second_dev}, device_id_type=pl.DeviceIdType.MESH)
+            src_ref=comb.at[t, half, second_g], dst_ref=rb2.at[t, half, 2], send_sem=rs_send.at[1],
+            recv_sem=rs_recv.at[t, half], device_id={'cp': second_dev}, device_id_type=pl.DeviceIdType.MESH)
 
     def combine_relayed(t, half, late):
         d2d(t, half, late).wait_recv()
@@ -389,56 +385,47 @@
 
     @pl.when(cy == 0)
     def _():
-        rs(1, 1, 1).wait_recv()
+        rs_sum(1, 1, 1).wait_recv()
         put_total(1, 1, comb[1, 1, 0] + rb2[1, 1, 1])
 
     @pl.when(cy == 1)
     def _():
-        for g in (1, 2, 3):
-            rs(1, 1, g).wait_recv()
+        rs_sum(1, 1, 3).wait_recv()
         put_total(1, 1, (comb[1, 1, 0] + rb2[1, 1, 1]) + (rb2[1, 1, 2] + rb2[1, 1, 3]))
 
     for t, half in UNITS[1:3]:
-        to_first(t, half, 1).wait_recv()
-        to_second(t, half).wait_recv()
+        rs_sum(t, half, 2).wait_recv()
         put_total(t, half, comb[t, half, 0] + (rb2[t, half, 1] + rb2[t, half, 2]))
-    for g in (3, 1, 2):
-        rs(0, 0, g).wait_recv()
+    rs_sum(0, 0, 3).wait_recv()
     put_total(0, 0, (comb[0, 0, 0] + rb2[0, 0, 1]) + (rb2[0, 0, 2] + rb2[0, 0, 3]))
 
     doc_sum.wait_send()
     for t in range(2):
-        for g in range(4):
-            kv_send_own(t, g).wait_send()
+        four = kv_s.at[t, :, 0:4 * PIECE, :]
+        rcopy(four, four, kv_send.at[t], kv_recv.at[t, 0], 1).wait_send()
 
     @pl.when(core == 1)
     def _():
         for t in range(2):
-            six = kv_s.at[t, :, 0:6 * PIECE, :]
-            rcopy(six, six, kv_pass.at[t], kv_recv.at[t, 0], 1).wait_send()
+            kv_sum(t, 6).wait_send()
 
     for t in range(2):
         d2d(t, 0, 0).wait_send()
-    rs(1, 1, 1).wait_send()
 
     @pl.when(cy == 0)
     def _():
         for t in range(2):
             d2d(t, 1, 0).wait_send()
-        for g in range(2, 4):
-            rs(1, 1, g).wait_send()
+        rs_sum(1, 1, 3).wait_send()
 
     @pl.when(cy == 1)
     def _():
         for t in range(2):
             d2d(t, 1, 1).wait_send()
-
-    for t, half in UNITS[1:3]:
-        to_first(t, half, 0).wait_send()
-        to_first(t, half, 1).wait_send()
-        to_second(t, half).wait_send()
-    for g in (1, 2, 3):
-        rs(0, 0, g).wait_send()
+        rs_sum(1, 1, 1).wait_send()
+
+    nine = s_s.at[0:9 * PIECE * E // (3 * HALF), :]
+    rcopy(nine, nine, rs_send.at[1], rs_recv.at[0, 0], 2).wait_send()
 
 
 FIN = ((0, 1536), (1536, 2560), (2560, 3584))
@@ -484,8 +471,8 @@
                 V((2, 2, 4, 2, PIECE, E), F32),
                 V((2, 2, 4, PIECE, E), F32), V((2, 2, 4, PIECE, E), F32), V((2, 2, 4, PIECE, E), F32), V((2, 2, PIECE, E), F32),
                 dma((len(KPARTS), 3)), dma((3,)), dma((2,)), dma, dma,
-                dma, dma, dma((2, 4)), dma((2, 7)), dma((2,)),
-                dma((2, 2)), dma((2, 2)), dma((2, 2, 3)), dma((2, 2, 3)),
+                dma, dma, dma((2,)), dma((2, 2)), dma((2,)),
+                dma((2, 2)), dma((2, 2)), dma((2,)), dma((2, 2)), dma((2,)),
             ],
             compiler_params=pltpu.CompilerParams(collective_id=0, has_side_effects=True,
                                                  vmem_limit_bytes=50 * 1024 * 1024),

time: 26.4 us -> 26.1 us (0.989)
  Pallas kernels: 25.5 us -> 25.2 us
    pallas_call x1, Pallas kernels: 23.9 us -> 23.6 us  [local_layer(): pl.pallas_call(main_kernel, out_shape=(V((TOK, D), BF16), V((TOK, D), F32...]
where the time goes in v8:
time: 26.1 us; the launch traced here: 26 us
  Pallas kernels  25.2 us (97%)
  between operations  0.8 us (3%)
    pallas_call x1, Pallas kernels, local_layer(): pl.pallas_call(main_kernel, out_shape=(V((TOK, D), BF16), V((TOK, D), F32...  23.6 us
    pallas_call x1, Pallas kernels, local_layer(): pl.pallas_call(final_kernel, out_shape=(sds((TOK, D), BF16), sds((TOK, D)...  1.56 us

profile of v8, /device:TPU:0, one launch (start us, length us, event | category | flops | bytes accessed | tf_op | source)
XLA Modules:
  0.0 26.0 jit_solution(1829619143726564969)
XLA Ops:
  0.6 23.6 %shard_map.86 = (bf16[192,3584]{1,0:T(8,128)(2,1)S(1)}, f32[192,3584]{1,0:T(8,128)S(1)}, bf16[192,256]{1,0:T(8,128)(2,1)S(1)}, bf16[2,3584,128]{2,1,0:T(8,128)(2,1)S(1)}) custom-call(bf16[192,3584]{1,0:T(8,128)(2,1)} %x_hbm.1, bf16[192,3584]{1,0:T(8,128)(2,1)} %dy_hbm.1, s32[1,192]{1,0:T(1,128)} %bitcast.9, bf16[7,3584,128]{2,1,0:T(8,128)(2,1)} %bitcast.5, ...), custom_call_target="tpu_custom_call" | custom-call | tf_op jit(solution)/shard_map/pallas_call | solution.py:458
  24.3 1.6 %shard_map.87 = (bf16[192,3584]{1,0:T(8,128)(2,1)}, bf16[192,3584]{1,0:T(8,128)(2,1)}) custom-call(bf16[192,3584]{1,0:T(8,128)(2,1)S(1)} %get-tuple-element.6.y_s, f32[192,3584]{1,0:T(8,128)S(1)} %get-tuple-element.7.dx_s, bf16[192,256]{1,0:T(8,128)(2,1)S(1)} %get-tuple-element.8.dkv_s, bf16[2,3584,128]{2,1,0:T(8,128)(2,1)S(1)} %get-tuple-element.9.wkv_s), custom_call_target="tpu_custom_call" | custom-call | tf_op jit(solution)/shard_map/pallas_call | solution.py:481

commit v9 on v8

--- a/solution.py
+++ b/solution.py
@@ -123,7 +123,7 @@
         return rcopy(blks, blks, kv_pass.at[t], kv_recv.at[t, 1], 1)
 
     for t in range(2):
-        for g in (3, 1, 2, 0):
+        for g in (1, 2, 3, 0):
             kv_send_own(t, g).start()
 
     def hand_on(t):

time: 26.1 us -> 26 us (level)
  no operation moved by 1% of the time
where the time goes in v9:
time: 26 us; the launch traced here: 25.9 us
  Pallas kernels  25.1 us (97%)
  between operations  0.8 us (3%)
    pallas_call x1, Pallas kernels, local_layer(): pl.pallas_call(main_kernel, out_shape=(V((TOK, D), BF16), V((TOK, D), F32...  23.6 us
    pallas_call x1, Pallas kernels, local_layer(): pl.pallas_call(final_kernel, out_shape=(sds((TOK, D), BF16), sds((TOK, D)...  1.56 us

profile of v9, /device:TPU:0, one launch (start us, length us, event | category | flops | bytes accessed | tf_op | source)
XLA Modules:
  0.0 25.9 jit_solution(5814415247929280449)
XLA Ops:
  0.6 23.6 %shard_map.86 = (bf16[192,3584]{1,0:T(8,128)(2,1)S(1)}, f32[192,3584]{1,0:T(8,128)S(1)}, bf16[192,256]{1,0:T(8,128)(2,1)S(1)}, bf16[2,3584,128]{2,1,0:T(8,128)(2,1)S(1)}) custom-call(bf16[192,3584]{1,0:T(8,128)(2,1)} %x_hbm.1, bf16[192,3584]{1,0:T(8,128)(2,1)} %dy_hbm.1, s32[1,192]{1,0:T(1,128)} %bitcast.9, bf16[7,3584,128]{2,1,0:T(8,128)(2,1)} %bitcast.5, ...), custom_call_target="tpu_custom_call" | custom-call | tf_op jit(solution)/shard_map/pallas_call | solution.py:458
  24.2 1.6 %shard_map.87 = (bf16[192,3584]{1,0:T(8,128)(2,1)}, bf16[192,3584]{1,0:T(8,128)(2,1)}) custom-call(bf16[192,3584]{1,0:T(8,128)(2,1)S(1)} %get-tuple-element.6.y_s, f32[192,3584]{1,0:T(8,128)S(1)} %get-tuple-element.7.dx_s, bf16[192,256]{1,0:T(8,128)(2,1)S(1)} %get-tuple-element.8.dkv_s, bf16[2,3584,128]{2,1,0:T(8,128)(2,1)S(1)} %get-tuple-element.9.wkv_s), custom_call_target="tpu_custom_call" | custom-call | tf_op jit(solution)/shard_map/pallas_call | solution.py:481

commit v10 on v9

--- a/solution.py
+++ b/solution.py
@@ -375,9 +375,6 @@
     pass_on(1, 0)
     y_part(1792, D)
     pass_on(0, 1)
-    for i in range(D // NY):
-        dx_s[:, i * NY:(i + 1) * NY] = dot(dq_s[...], side_by_side(wq_s, 0, HEADS, i * NY, (i + 1) * NY), NT)
-
     def put_total(t, half, tot):
         if t == 0:
             tot = tot * k_scale
@@ -392,6 +389,9 @@
     def _():
         rs_sum(1, 1, 3).wait_recv()
         put_total(1, 1, (comb[1, 1, 0] + rb2[1, 1, 1]) + (rb2[1, 1, 2] + rb2[1, 1, 3]))
+
+    for i in range(D // NY):
+        dx_s[:, i * NY:(i + 1) * NY] = dot(dq_s[...], side_by_side(wq_s, 0, HEADS, i * NY, (i + 1) * NY), NT)
 
     for t, half in UNITS[1:3]:
         rs_sum(t, half, 2).wait_recv()

time: 26 us -> 26 us (level)
  no operation moved by 1% of the time
where the time goes in v10:
time: 26 us; the launch traced here: 25.9 us
  Pallas kernels  25.1 us (97%)
  between operations  0.8 us (3%)
    pallas_call x1, Pallas kernels, local_layer(): pl.pallas_call(main_kernel, out_shape=(V((TOK, D), BF16), V((TOK, D), F32...  23.6 us
    pallas_call x1, Pallas kernels, local_layer(): pl.pallas_call(final_kernel, out_shape=(sds((TOK, D), BF16), sds((TOK, D)...  1.56 us

profile of v10, /device:TPU:0, one launch (start us, length us, event | category | flops | bytes accessed | tf_op | source)
XLA Modules:
  0.0 25.9 jit_solution(11679105344039840591)
XLA Ops:
  0.6 23.6 %shard_map.86 = (bf16[192,3584]{1,0:T(8,128)(2,1)S(1)}, f32[192,3584]{1,0:T(8,128)S(1)}, bf16[192,256]{1,0:T(8,128)(2,1)S(1)}, bf16[2,3584,128]{2,1,0:T(8,128)(2,1)S(1)}) custom-call(bf16[192,3584]{1,0:T(8,128)(2,1)} %x_hbm.1, bf16[192,3584]{1,0:T(8,128)(2,1)} %dy_hbm.1, s32[1,192]{1,0:T(1,128)} %bitcast.9, bf16[7,3584,128]{2,1,0:T(8,128)(2,1)} %bitcast.5, ...), custom_call_target="tpu_custom_call" | custom-call | tf_op jit(solution)/shard_map/pallas_call | solution.py:458
  24.2 1.6 %shard_map.87 = (bf16[192,3584]{1,0:T(8,128)(2,1)}, bf16[192,3584]{1,0:T(8,128)(2,1)}) custom-call(bf16[192,3584]{1,0:T(8,128)(2,1)S(1)} %get-tuple-element.6.y_s, f32[192,3584]{1,0:T(8,128)S(1)} %get-tuple-element.7.dx_s, bf16[192,256]{1,0:T(8,128)(2,1)S(1)} %get-tuple-element.8.dkv_s, bf16[2,3584,128]{2,1,0:T(8,128)(2,1)S(1)} %get-tuple-element.9.wkv_s), custom_call_target="tpu_custom_call" | custom-call | tf_op jit(solution)/shard_map/pallas_call | solution.py:481
